TPU v7x, 256 devices: a whole 4x4x8 slice. The times are simulated.
256 devices in a mesh: group: 32 (over x, z), tensor: 8 (over y, core).
Axes of the slice: x: 4, y: 4, z: 8, core: 2. Of those that a mesh axis runs over, the one named last changes fastest.
Arguments:
- queries: bfloat16 [1024, 64, 5120], P('group', None, 'tensor'), may hold values from -15 to 15
- prefix_keys: bfloat16 [64, 1024, 1024], P('group', None, 'tensor'), may hold values from -200 to 200
- prefix_values: bfloat16 [64, 1024, 1024], P('group', None, 'tensor'), may hold values from -6 to 6
- slot_of_prompt: int32 [64], replicated, may hold values from 0 to 63, as said below
- prompt_of: int32 [1024], P('group'), may hold values from 0 to 63, as said below
- lengths: int32 [1024], P('group'), may hold values from 1 to 64
Outputs:
- attended: bfloat16 [1024, 64, 5120], P('group', 'tensor')
Inputs may be any that keep to these rules, and one draw needn't show every extreme that they name: A permutation: prompt p's keys and values lie in row slot_of_prompt[p] of the prefix arrays, and that row belongs to group index slot_of_prompt[p] // 2. `prompt_of`: of the 32 completions on one group index, at most 2 have prompts cached on any one group index, and on every group index some group index caches the prompts of exactly 2 of them.
All inputs are finite; a program needn't handle non-finite values.
Results may differ from a plain program's by a relative error of at most 0.012.
Values may be sent and summed in bfloat16 or wider, within the bound.
No kernel may reach another device: no remote copies, remote signals or barrier semaphores. Data moves between devices by JAX's collectives and lax.ppermute only.
A program may use at most 64 MiB of HBM per device.

v0:
```python
import math

import jax
import jax.numpy as jnp
from jax import lax
from jax.sharding import PartitionSpec as P

HEAD = 128
CAPC = 2


rotary_base = 1000000.0
block_items = 8


def exchange_in_groups(array, axis, split_dim, concat_dim, work, item_dim, out_dim):
    items = jax.tree.leaves(array)[0].shape[item_dim]
    count = 2 if items % 2 == 0 else 1
    gathered = []
    for k in range(count):
        group = jax.tree.map(
            lambda a: lax.slice_in_dim(
                a, k * (items // count), (k + 1) * (items // count), axis=item_dim
            ),
            array,
        )
        gathered.append(
            work(
                lax.all_to_all(
                    group, axis, split_axis=split_dim, concat_axis=concat_dim, tiled=True
                )
            )
        )
    return jax.tree.map(lambda *parts: jnp.concatenate(parts, axis=out_dim), *gathered)


def rotary(head_rows, positions):
    half_dim = head_rows.shape[-1] // 2
    frequencies = rotary_base ** (
        -(jnp.arange(half_dim, dtype=jnp.float32) * 2.0 / head_rows.shape[-1])
    )
    angles = positions[:, None] * frequencies[None, :]
    cos_table = jnp.cos(angles)[:, None, :]
    sin_table = jnp.sin(angles)[:, None, :]
    first_half = head_rows[..., :half_dim]
    second_half = head_rows[..., half_dim:]
    return jnp.concatenate(
        [
            first_half * cos_table - second_half * sin_table,
            second_half * cos_table + first_half * sin_table,
        ],
        axis=-1,
    )


def attend_block(query_block, tag_block, cached_keys, cached_values, kv_local):
    slot_items, comp_rows, feature_width = query_block.shape
    cached, prefix_rows, kv_width = cached_keys.shape
    heads_local = feature_width // HEAD
    per_kv = heads_local // kv_local
    selector = (tag_block[:, None] == jnp.arange(cached).astype(jnp.bfloat16)[None, :]).astype(
        jnp.bfloat16
    )
    chosen_keys = jnp.einsum(
        "bc,cpw->bpw", selector, cached_keys, preferred_element_type=jnp.float32
    ).astype(jnp.bfloat16)
    chosen_values = jnp.einsum(
        "bc,cpw->bpw", selector, cached_values, preferred_element_type=jnp.float32
    ).astype(jnp.bfloat16)
    grouped = query_block.reshape(slot_items, comp_rows, kv_local, per_kv, HEAD)
    key_heads = chosen_keys.reshape(slot_items, prefix_rows, kv_local, HEAD)
    value_heads = chosen_values.reshape(slot_items, prefix_rows, kv_local, HEAD)
    scores = jnp.einsum(
        "brkgd,bpkd->bkgrp", grouped, key_heads, preferred_element_type=jnp.float32
    ) * (1.0 / math.sqrt(HEAD))
    peak = jnp.max(scores, axis=-1, keepdims=True)
    weights = jnp.exp(scores - peak)
    denominator = jnp.sum(weights, axis=-1)
    probabilities = weights.astype(jnp.bfloat16)
    weighted = jnp.einsum(
        "bkgrp,bpkd->brkgd", probabilities, value_heads, preferred_element_type=jnp.float32
    )
    attended = weighted / jnp.transpose(denominator, (0, 3, 1, 2))[..., None]
    return attended.astype(jnp.bfloat16).reshape(slot_items, comp_rows, feature_width)


def attend_items(query_items, cache_tags, cached_keys, cached_values, kv_local):
    total_items, comp_rows, feature_width = query_items.shape
    group_size = min(block_items, total_items)
    padding = -total_items % group_size
    query_items = jnp.pad(query_items, ((0, padding), (0, 0), (0, 0)))
    cache_tags = jnp.pad(cache_tags, (0, padding), constant_values=-1)
    padded_items = total_items + padding
    query_blocks = query_items.reshape(
        padded_items // group_size, group_size, comp_rows, feature_width
    )
    tag_blocks = cache_tags.reshape(padded_items // group_size, group_size)

    def compute(pair):
        return attend_block(pair[0], pair[1], cached_keys, cached_values, kv_local)

    results = lax.map(compute, (query_blocks, tag_blocks)).reshape(
        padded_items, comp_rows, feature_width
    )
    return results[:total_items]


def local(queries, prefix_keys, prefix_values, slot_of_prompt, prompt_of, lengths):
    groups = lax.axis_size("group")
    completions_here, comp_rows, feature_width = queries.shape
    cached = prefix_keys.shape[0]
    kv_local = prefix_keys.shape[2] // HEAD
    heads_local = feature_width // HEAD
    positions = (prefix_keys.shape[1] + jnp.arange(comp_rows)).astype(jnp.float32)
    roped = rotary(
        queries.astype(jnp.float32).reshape(completions_here, comp_rows, heads_local, HEAD),
        positions,
    )
    roped = roped.astype(jnp.bfloat16).reshape(completions_here, comp_rows, feature_width)
    cache_rows = slot_of_prompt[prompt_of]
    owner_group = cache_rows // cached
    local_rows = cache_rows % cached
    serial = jnp.arange(completions_here)
    earlier = (owner_group[None, :] == owner_group[:, None]) & (serial[None, :] < serial[:, None])
    arrival = jnp.sum(earlier.astype(jnp.int32), axis=1)
    destination = owner_group * CAPC + arrival
    slot_count = groups * CAPC
    matches = destination[None, :] == jnp.arange(slot_count)[:, None]
    filled = jnp.any(matches, axis=1)
    source_index = jnp.sum(jnp.where(matches, serial[None, :], 0), axis=1)
    outgoing = jnp.where(filled[:, None, None], roped[source_index], jnp.zeros((), jnp.bfloat16))
    outgoing = outgoing.reshape(groups, CAPC, comp_rows, feature_width)
    cache_tags = (
        jnp.where(filled, local_rows[source_index], -1).astype(jnp.bfloat16).reshape(groups, CAPC)
    )

    def serve_slots(pieces):
        received, slot_tags = pieces
        senders, slot_items = slot_tags.shape
        attended = attend_items(
            received.reshape(senders * slot_items, comp_rows, feature_width),
            slot_tags.reshape(senders * slot_items),
            prefix_keys,
            prefix_values,
            kv_local,
        )
        attended = attended.reshape(senders, slot_items, comp_rows, feature_width)
        result = lax.all_to_all(attended, "group", split_axis=0, concat_axis=0, tiled=True)
        return result

    returned = exchange_in_groups((outgoing, cache_tags), "group", 0, 0, serve_slots, 1, 1)
    flattened = returned.reshape(slot_count, returned.shape[2], returned.shape[3])
    own_rows = flattened[destination]
    row_share = comp_rows // lax.axis_size("tensor")
    attended_rows = lax.all_to_all(own_rows, "tensor", split_axis=1, concat_axis=2, tiled=True)
    row_positions = lax.axis_index("tensor") * row_share + jnp.arange(row_share)
    live_rows = row_positions[None, :] < lengths[:, None]
    return jnp.where(live_rows[:, :, None], attended_rows, jnp.zeros((), jnp.bfloat16))


def solution(mesh):
    placed = (
        P("group", None, "tensor"),
        P("group", None, "tensor"),
        P("group", None, "tensor"),
        P(),
        P("group"),
        P("group"),
    )
    return jax.shard_map(
        local, mesh=mesh, in_specs=placed, out_specs=P("group", "tensor", None), check_vma=False
    )
```

profile of v0, /device:TPU:1, one launch (start us, length us, event | category | flops | bytes accessed | tf_op | source)
XLA Modules:
  0.0 396.0 jit_solution(16915176676404708598)
XLA Ops:
  4.0 11.9 %all-to-all-start = ((bf16[32,1,1]{2,1,0:T(2,128)(2,1)}), bf16[32,1,1]{2,1,0:T(2,128)(2,1)S(1)}, u32[]{:S(2)}, u32[]{:S(2)}) async-start(bf16[32,1,1]{2,1,0:T(2,128)(2,1)} %all_to_all.49), calls=%async_computation | async-start | bytes 32768 | tf_op jit(solution)/shard_map/all_to_all | solution.py:29
  15.9 7.2 %reshape.328 = f32[32,64,5,128]{3,2,1,0:T(8,128)} reshape(bf16[32,64,640]{2,1,0:T(8,128)(2,1)} %param.10) | data formatting | bytes 7864320 | tf_op jit(solution)/shard_map/reshape | solution.py:116
  23.3 7.4 %subtract_convert_fusion = (bf16[32,64,5,64]{3,2,1,0:T(8,128)(2,1)S(1)}, bf16[32,64,5,64]{3,2,1,0:T(8,128)(2,1)S(1)}) fusion(f32[32,64,5,128]{3,2,1,0:T(8,128)} %reshape.328, f32[64,64]{1,0:T(8,128)S(1)} %get-tuple-element.142, f32[64,64]{1,0:T(8,128)S(1)} %get-tuple-element.141), kind=kLoop, calls=%fused_computation.67 | loop fusion | flops 5242880 | bytes 7897088 | tf_op jit(solution)/shard_map/convert.1
  30.7 4.2 %pad_maximum_fusion.1 = bf16[32,64,5,128]{3,2,1,0:T(8,128)(2,1)} fusion(bf16[32,64,5,64]{3,2,1,0:T(8,128)(2,1)S(1)} %get-tuple-element.138, bf16[32,64,5,64]{3,2,1,0:T(8,128)(2,1)S(1)} %get-tuple-element.137), kind=kLoop, calls=%fused_computation.70 | loop fusion | flops 5242880 | bytes 5242880 | tf_op jit(solution)/shard_map/concatenate | solution.py:47
  34.8 6.0 %convert_element_type.69 = bf16[32,64,640]{2,1,0:T(8,128)(2,1)S(1)} reshape(bf16[32,64,5,128]{3,2,1,0:T(8,128)(2,1)} %pad_maximum_fusion.1) | data formatting | bytes 5242880 | tf_op jit(solution)/shard_map/convert_element_type | solution.py:119
  40.8 3.5 gather_fusion.2
  44.3 5.3 %broadcast_select_fusion = bf16[32,2,64,640]{3,2,1,0:T(8,128)(2,1)} fusion(bf16[32,2,64,640]{3,2,1,0:T(8,128)(2,1)} %bitcast.188, pred[32,2]{1,0:T(8,128)(4,1)S(1)} %broadcast_in_dim.78), kind=kLoop, calls=%fused_computation.69 | loop fusion | flops 2621440 | bytes 10485824 | tf_op jit(solution)/shard_map/jit(_where)/select_n | solution.py:131
  50.4 9.2 %all-to-all-start.3 = ((bf16[32,1,1]{2,1,0:T(2,128)(2,1)}), bf16[32,1,1]{2,1,0:T(2,128)(2,1)S(1)}, u32[]{:S(2)}, u32[]{:S(2)}) async-start(bf16[32,1,1]{2,1,0:T(2,128)(2,1)} %all_to_all.50), calls=%async_computation.3 | async-start | bytes 32768 | tf_op jit(solution)/shard_map/all_to_all | solution.py:29
  59.6 5.4 %fusion.66 = (bf16[32,1,64,640]{3,2,1,0:T(8,128)(2,1)}, bf16[32,1,64,640]{3,2,1,0:T(8,128)(2,1)}) fusion(bf16[32,2,64,640]{3,2,1,0:T(8,128)(2,1)} %broadcast_select_fusion), kind=kLoop, calls=%fused_computation.107 | loop fusion | bytes 10485760 | tf_op jit(solution)/shard_map/slice | solution.py:22
  65.0 3.3 all-to-all-done.3
  68.3 6.2 %all-to-all-start.1 = ((bf16[32,1,64,640]{3,2,1,0:T(8,128)(2,1)}), bf16[32,1,64,640]{3,2,1,0:T(8,128)(2,1)}, u32[]{:S(2)}, u32[]{:S(2)}) async-start(bf16[32,1,64,640]{3,2,1,0:T(8,128)(2,1)} %get-tuple-element.139), calls=%async_computation.1 | async-start | bytes 5242880 | tf_op jit(solution)/shard_map/all_to_all | solution.py:29
  77.2 57.4 %all-to-all-done.1 = bf16[32,1,64,640]{3,2,1,0:T(8,128)(2,1)} async-done(((bf16[32,1,64,640]{3,2,1,0:T(8,128)(2,1)}), bf16[32,1,64,640]{3,2,1,0:T(8,128)(2,1)}, u32[]{:S(2)}, u32[]{:S(2)}) %all-to-all-start.1) | async-done | bytes 2621472 | tf_op jit(solution)/shard_map/all_to_all | solution.py:29
  134.5 6.9 %all-to-all-start.4 = ((bf16[32,1,64,640]{3,2,1,0:T(8,128)(2,1)}), bf16[32,1,64,640]{3,2,1,0:T(8,128)(2,1)}, u32[]{:S(2)}, u32[]{:S(2)}) async-start(bf16[32,1,64,640]{3,2,1,0:T(8,128)(2,1)} %get-tuple-element.140), calls=%async_computation.4 | async-start | bytes 5242880 | tf_op jit(solution)/shard_map/all_to_all | solution.py:29
  141.4 1.9 broadcast.272.clone.1
  143.3 59.1 %while.20 = (s32[]{:T(128)}, bf16[4,8,64,640]{3,2,1,0:T(8,128)(2,1)}, bf16[4,8]{1,0:T(4,128)(2,1)S(1)}, bf16[2,1024,128]{2,0,1:T(2,128)(2,1)}, bf16[2,1024,128]{...) while((s32[]{:T(128)}, bf16[4,8,64,640]{3,2,1,0:T(8,128)(2,1)}, ...), condition=%wide.region_6.7_spmd, body=%wide.region_3.6_spmd.sunk | while | flops 1374284928 | bytes 55102196 | solution.py:102
  144.6 2.0 constant_dynamic-slice_fusion.6
  150.0 2.0 fusion.94
  153.2 2.7 divide_convert_fusion.4
  159.4 2.0 constant_dynamic-slice_fusion.6
  164.8 2.0 fusion.94
  168.0 2.7 divide_convert_fusion.4
  174.2 2.0 constant_dynamic-slice_fusion.6
  179.6 2.0 fusion.94
  182.8 2.7 divide_convert_fusion.4
  188.9 2.0 constant_dynamic-slice_fusion.6
  194.3 2.0 fusion.94
  197.6 2.7 divide_convert_fusion.4
  202.4 9.3 %all-to-all-start.2 = ((bf16[32,1,64,640]{3,2,1,0:T(8,128)(2,1)}), bf16[32,1,64,640]{3,2,1,0:T(8,128)(2,1)}, u32[]{:S(2)}, u32[]{:S(2)}) async-start(bf16[32,1,64,640]{3,2,1,0:T(8,128)(2,1)} %bitcast.192), calls=%async_computation.2 | async-start | bytes 5242880 | tf_op jit(solution)/shard_map/all_to_all | solution.py:148
  213.6 59.0 %while.21 = (s32[]{:T(128)}, bf16[4,8,64,640]{3,2,1,0:T(8,128)(2,1)}, bf16[4,8]{1,0:T(4,128)(2,1)S(1)}, bf16[2,1024,128]{2,0,1:T(2,128)(2,1)}, bf16[2,1024,128]{...) while((s32[]{:T(128)}, bf16[4,8,64,640]{3,2,1,0:T(8,128)(2,1)}, ...), condition=%wide.region_10.11_spmd, body=%wide.region_7.10_spmd.sunk | while | flops 1374284928 | bytes 55102196 | solution.py:102
  214.8 2.0 constant_dynamic-slice_fusion.7
  220.3 2.0 fusion.102
  223.5 2.7 divide_convert_fusion.5
  229.6 2.0 constant_dynamic-slice_fusion.7
  235.0 2.0 fusion.102
  238.2 2.7 divide_convert_fusion.5
  244.3 2.0 constant_dynamic-slice_fusion.7
  249.8 2.0 fusion.102
  253.0 2.7 divide_convert_fusion.5
  259.1 2.0 constant_dynamic-slice_fusion.7
  264.5 2.0 fusion.102
  267.7 2.7 divide_convert_fusion.5
  272.6 9.0 %all-to-all-start.5 = ((bf16[32,1,64,640]{3,2,1,0:T(8,128)(2,1)}), bf16[32,1,64,640]{3,2,1,0:T(8,128)(2,1)S(1)}, u32[]{:S(2)}, u32[]{:S(2)}) async-start(bf16[32,1,64,640]{3,2,1,0:T(8,128)(2,1)} %bitcast.191), calls=%async_computation.5 | async-start | bytes 5242880 | tf_op jit(solution)/shard_map/all_to_all | solution.py:148
  281.6 58.4 %all-to-all-done.5 = bf16[32,1,64,640]{3,2,1,0:T(8,128)(2,1)S(1)} async-done(((bf16[32,1,64,640]{3,2,1,0:T(8,128)(2,1)}), bf16[32,1,64,640]{3,2,1,0:T(8,128)(2,1)S(1)}, u32[]{:S(2)}, u32[]{:S(2)}) %all-to-all-start.5) | async-done | bytes 2621472 | tf_op jit(solution)/shard_map/all_to_all | solution.py:148
  340.1 4.6 %pad_maximum_fusion = bf16[32,2,64,640]{3,2,1,0:T(8,128)(2,1)} fusion(bf16[32,1,64,640]{3,2,1,0:T(8,128)(2,1)S(1)} %all-to-all-done.5, bf16[32,1,64,640]{3,2,1,0:T(8,128)(2,1)} %all-to-all-done.2), kind=kLoop, calls=%fused_computation.68 | loop fusion | flops 2621440 | bytes 10485760 | tf_op jit(solution)/shard_map/concatenate | solution.py:34
  344.7 3.5 gather_fusion.3
  348.2 3.0 copy.58
  351.2 10.3 %all-to-all-start.6 = ((bf16[32,64,640]{2,0,1:T(8,128)(2,1)}), bf16[32,64,640]{2,0,1:T(8,128)(2,1)S(1)}, u32[]{:S(2)}, u32[]{:S(2)}) async-start(bf16[32,64,640]{2,0,1:T(8,128)(2,1)} %copy.58), calls=%async_computation.6 | async-start | bytes 5242880 | tf_op jit(solution)/shard_map/all_to_all | solution.py:155
  361.6 31.7 %all-to-all-done.6 = bf16[32,64,640]{2,0,1:T(8,128)(2,1)S(1)} async-done(((bf16[32,64,640]{2,0,1:T(8,128)(2,1)}), bf16[32,64,640]{2,0,1:T(8,128)(2,1)S(1)}, u32[]{:S(2)}, u32[]{:S(2)}) %all-to-all-start.6) | async-done | bytes 2621472 | tf_op jit(solution)/shard_map/all_to_all | solution.py:155
  (174 shorter events, 76.1 us)
Async XLA Ops:
  0.0 0.7 copy-start
  1.4 0.5 copy-start.11
  1.6 0.5 copy-start.13
  4.0 46.4 %all-to-all-start = ((bf16[32,1,1]{2,1,0:T(2,128)(2,1)}), bf16[32,1,1]{2,1,0:T(2,128)(2,1)S(1)}, u32[]{:S(2)}, u32[]{:S(2)}) async-start(bf16[32,1,1]{2,1,0:T(2,128)(2,1)} %all_to_all.49), calls=%async_computation | async-start | bytes 32768 | tf_op jit(solution)/shard_map/all_to_all | solution.py:29
  50.4 17.9 %all-to-all-start.3 = ((bf16[32,1,1]{2,1,0:T(2,128)(2,1)}), bf16[32,1,1]{2,1,0:T(2,128)(2,1)S(1)}, u32[]{:S(2)}, u32[]{:S(2)}) async-start(bf16[32,1,1]{2,1,0:T(2,128)(2,1)} %all_to_all.50), calls=%async_computation.3 | async-start | bytes 32768 | tf_op jit(solution)/shard_map/all_to_all | solution.py:29
  65.0 9.5 %copy-start.8 = (bf16[2,1024,128]{2,1,0:T(8,128)(2,1)S(1)}, bf16[2,1024,128]{2,1,0:T(8,128)(2,1)}, u32[]{:S(2)}) copy-start(bf16[2,1024,128]{2,1,0:T(8,128)(2,1)} %param.12) | copy-start | bytes 1572868
  65.0 10.9 %copy-start.9 = (bf16[2,1024,128]{2,1,0:T(8,128)(2,1)S(1)}, bf16[2,1024,128]{2,1,0:T(8,128)(2,1)}, u32[]{:S(2)}) copy-start(bf16[2,1024,128]{2,1,0:T(8,128)(2,1)} %param.11) | copy-start | bytes 1572868
  68.3 66.3 %all-to-all-start.1 = ((bf16[32,1,64,640]{3,2,1,0:T(8,128)(2,1)}), bf16[32,1,64,640]{3,2,1,0:T(8,128)(2,1)}, u32[]{:S(2)}, u32[]{:S(2)}) async-start(bf16[32,1,64,640]{3,2,1,0:T(8,128)(2,1)} %get-tuple-element.139), calls=%async_computation.1 | async-start | bytes 5242880 | tf_op jit(solution)/shard_map/all_to_all | solution.py:29
  134.5 67.9 %all-to-all-start.4 = ((bf16[32,1,64,640]{3,2,1,0:T(8,128)(2,1)}), bf16[32,1,64,640]{3,2,1,0:T(8,128)(2,1)}, u32[]{:S(2)}, u32[]{:S(2)}) async-start(bf16[32,1,64,640]{3,2,1,0:T(8,128)(2,1)} %get-tuple-element.140), calls=%async_computation.4 | async-start | bytes 5242880 | tf_op jit(solution)/shard_map/all_to_all | solution.py:29
  143.3 1.2 copy-start.4
  150.0 2.0 copy-start.2
  155.9 2.2 copy-start.5
  158.1 1.2 copy-start.4
  164.8 2.0 copy-start.2
  170.7 2.2 copy-start.5
  172.9 1.2 copy-start.4
  179.6 2.0 copy-start.2
  185.5 2.2 copy-start.5
  187.7 1.2 copy-start.4
  194.3 2.0 copy-start.2
  200.2 2.2 copy-start.5
  202.4 70.2 %all-to-all-start.2 = ((bf16[32,1,64,640]{3,2,1,0:T(8,128)(2,1)}), bf16[32,1,64,640]{3,2,1,0:T(8,128)(2,1)}, u32[]{:S(2)}, u32[]{:S(2)}) async-start(bf16[32,1,64,640]{3,2,1,0:T(8,128)(2,1)} %bitcast.192), calls=%async_computation.2 | async-start | bytes 5242880 | tf_op jit(solution)/shard_map/all_to_all | solution.py:148
  213.6 1.2 copy-start.6
  220.3 2.0 copy-start.3
  226.2 2.2 copy-start.7
  228.3 1.2 copy-start.6
  235.0 2.0 copy-start.3
  240.9 2.2 copy-start.7
  243.1 1.2 copy-start.6
  249.7 2.0 copy-start.3
  255.7 2.2 copy-start.7
  257.8 1.2 copy-start.6
  264.5 2.0 copy-start.3
  270.4 2.2 copy-start.7
  272.6 9.0 %copy-start.12 = (s32[32]{0:T(128)S(1)}, s32[32]{0:T(128)}, u32[]{:S(2)}) copy-start(s32[32]{0:T(128)} %copy-done.11) | copy-start | bytes 388
  272.6 9.0 %copy-start.14 = (s32[32]{0:T(128)S(1)}, s32[32]{0:T(128)}, u32[]{:S(2)}) copy-start(s32[32]{0:T(128)} %copy-done.13) | copy-start | bytes 388
  272.6 67.5 %all-to-all-start.5 = ((bf16[32,1,64,640]{3,2,1,0:T(8,128)(2,1)}), bf16[32,1,64,640]{3,2,1,0:T(8,128)(2,1)S(1)}, u32[]{:S(2)}, u32[]{:S(2)}) async-start(bf16[32,1,64,640]{3,2,1,0:T(8,128)(2,1)} %bitcast.191), calls=%async_computation.5 | async-start | bytes 5242880 | tf_op jit(solution)/shard_map/all_to_all | solution.py:148
  348.2 13.4 %copy-start.10 = (s32[32]{0:T(128)S(1)}, s32[32]{0:T(128)}, u32[]{:S(2)}) copy-start(s32[32]{0:T(128)} %param.15) | copy-start | bytes 388
  351.2 42.2 %all-to-all-start.6 = ((bf16[32,64,640]{2,0,1:T(8,128)(2,1)}), bf16[32,64,640]{2,0,1:T(8,128)(2,1)S(1)}, u32[]{:S(2)}, u32[]{:S(2)}) async-start(bf16[32,64,640]{2,0,1:T(8,128)(2,1)} %copy.58), calls=%async_computation.6 | async-start | bytes 5242880 | tf_op jit(solution)/shard_map/all_to_all | solution.py:155
  393.4 2.6 copy-start.1
where the time goes:
time: 397 us; the launch traced here: 396 us
  waiting for transfers between devices  151 us (38%)
  local copies, waits for them, and re-layouts  86.6 us (22%)
  starting transfers between devices  62.8 us (16%)
  matrix products  53.5 us (13%)
  other arithmetic  41.2 us (10%)
    all_to_all x4, waiting for transfers between devices, exchange_in_groups(): lax.all_to_all(group, axis, split_axis=split_dim, concat_axis=concat_dim,...  60.7 us
    all_to_all x2, waiting for transfers between devices, serve_slots(): lax.all_to_all(attended, 'group', split_axis=0, concat_axis=0, tiled=True)  58.5 us
    all_to_all x4, starting transfers between devices, exchange_in_groups(): lax.all_to_all(group, axis, split_axis=split_dim, concat_axis=concat_dim,...  34.1 us
    all_to_all x1, waiting for transfers between devices, local(): lax.all_to_all(own_rows, 'tensor', split_axis=1, concat_axis=2, tiled=True)  31.7 us
    dot_general x8, matrix products, attend_block(): jnp.einsum('bkgrp,bpkd->brkgd', probabilities, value_heads, preferred_ele...  21.4 us
    all_to_all x2, starting transfers between devices, serve_slots(): lax.all_to_all(attended, 'group', split_axis=0, concat_axis=0, tiled=True)  18.3 us
    another operation x10, local copies, waits for them, and re-layouts  18.1 us
    reduce_sum x8, other arithmetic, attend_block(): denominator = jnp.sum(weights, axis=-1)  16 us
  transfers between devices with their start and end apart: 7, of which 4 were waited for; matrix products, arithmetic and copies ran while one was open for 41% of the time, Pallas kernels for 0%

commit v1 on v0

v1 whole, which is shorter than its diff:
```python
import functools
import math

import jax
import jax.numpy as jnp
import numpy as np
from jax import lax
from jax.experimental import pallas as pl
from jax.experimental.pallas import tpu as pltpu
from jax.sharding import Mesh, PartitionSpec as P


HEAD = 128
CAPC = 2
ROTARY_BASE = 1000000.0
VMEM = 67043328
GROUPS_Z = 8
NEAR = 5
TURN = 4
TAIL = 16


def rotary_tables(first_position, rows):
    half = HEAD // 2
    frequencies = np.float32(ROTARY_BASE) ** (
        -(np.arange(half, dtype=np.float32) * np.float32(2.0) / np.float32(HEAD))
    )
    positions = np.arange(first_position, first_position + rows).astype(np.float32)
    angles = (positions[:, None] * frequencies[None, :]).astype(np.float32).astype(np.float64)
    cos, sin = np.cos(angles), np.sin(angles)
    return np.stack(
        [np.concatenate([cos, cos], axis=1), np.concatenate([-sin, sin], axis=1)]
    ).astype(np.float32)


def route(prompt, slot_ref, counts_ref, my_z):
    cache_slot = slot_ref[prompt]
    owner = cache_slot // 2
    row = cache_slot - owner * 2
    owner_x = owner // GROUPS_Z
    distance = lax.rem(owner - owner_x * GROUPS_Z - my_z + GROUPS_Z, GROUPS_Z)
    place = jnp.where(
        distance == 0, 0, jnp.where(distance <= 4, 2 * distance - 1, 2 * (GROUPS_Z - distance))
    )
    arrival = counts_ref[owner]
    counts_ref[owner] = arrival + 1
    return owner_x, place * CAPC + arrival, row


def pack_kernel(
    low, high, z_ref, slots_ref, prompts_ref, lengths_ref, queries_ref, tables_ref, sent_ref,
    held, staged, tables, tagged, slot_ref, prompt_ref, length_ref, counts_ref,
    to_x_ref, to_slot_ref, in_sems, out_sems, small_sems, tag_sem,
):
    items, rows, width = queries_ref.shape
    heads = width // HEAD
    tagging = sent_ref.shape[1] > (high - low) * rows
    smalls = [
        pltpu.make_async_copy(source, target, small_sems.at[index])
        for index, (source, target) in enumerate(
            (
                (slots_ref, slot_ref), (prompts_ref, prompt_ref), (lengths_ref, length_ref),
                (tables_ref, tables),
            )
        )
    ]
    for copy in smalls:
        copy.start()
    my_z = z_ref[0]
    for group in range(counts_ref.shape[0]):
        counts_ref[group] = 0
    line = lax.broadcasted_iota(jnp.int32, (8, HEAD), 0)
    lane = lax.broadcasted_iota(jnp.int32, (8, HEAD), 1)
    for copy in smalls:
        copy.wait()

    def plan(item, carry):
        found, tags = carry
        owner_x, slot, row = route(prompt_ref[item], slot_ref, counts_ref, my_z)
        inside = (slot >= low) & (slot < high)

        @pl.when(inside)
        def _():
            pltpu.make_async_copy(queries_ref.at[item], held.at[found], in_sems.at[found]).start()
            to_x_ref[found] = owner_x
            to_slot_ref[found] = slot - low

        if tagging:
            tags = jnp.where((line == owner_x) & (lane == slot), row + 1, tags)
            tags = jnp.where((line == owner_x) & (lane == slot + 64), length_ref[item], tags)
        return found + jnp.where(inside, 1, 0), tags

    found, tags = lax.fori_loop(0, items, plan, (0, jnp.zeros((8, HEAD), jnp.int32)))
    tail_copies = []
    if tagging:
        tags = tags.astype(jnp.float32)
        for owner_x in range(sent_ref.shape[0]):
            tagged[owner_x] = jnp.broadcast_to(tags[owner_x : owner_x + 1], (TAIL, HEAD)).astype(
                jnp.bfloat16
            )
            tail_copies.append(
                pltpu.make_async_copy(
                    tagged.at[owner_x],
                    sent_ref.at[owner_x, pl.ds((high - low) * rows, TAIL), pl.ds(0, HEAD)],
                    tag_sem.at[owner_x],
                )
            )
            tail_copies[-1].start()

    def turn(step, carry):
        for inner in range(TURN):
            index = step * TURN + inner

            @pl.when(index < found)
            def _(index=index):
                pltpu.make_async_copy(queries_ref.at[0], held.at[index], in_sems.at[index]).wait()

        for inner in range(TURN):
            index = step * TURN + inner
            for head in range(heads):
                part = held[index, :, head * HEAD : (head + 1) * HEAD].astype(jnp.float32)
                turned = part * tables[0] + pltpu.roll(part, HEAD // 2, 1) * tables[1]
                staged[index, :, head * HEAD : (head + 1) * HEAD] = turned.astype(jnp.bfloat16)
        for inner in range(TURN):
            index = step * TURN + inner

            @pl.when(index < found)
            def _(index=index):
                at = pl.ds(pl.multiple_of(to_slot_ref[index] * rows, rows), rows)
                pltpu.make_async_copy(
                    staged.at[index], sent_ref.at[to_x_ref[index], at], out_sems.at[index]
                ).start()

        return carry

    lax.fori_loop(0, (found + TURN - 1) // TURN, turn, 0)

    def leave(index, carry):
        pltpu.make_async_copy(
            staged.at[index], sent_ref.at[0, pl.ds(0, rows)], out_sems.at[index]
        ).wait()
        return carry

    lax.fori_loop(0, found, leave, 0)
    for copy in tail_copies:
        copy.wait()


def attend_kernel(first_slot, sent_slot, tags_ref, sent_ref, after_ref, *refs):
    (
        *cache_refs, out_ref, held, staged, keys, values, even_scores, odd_scores,
        even_peak, odd_peak, at_ref, cache_ref, length_ref, in_sems, out_sems, cache_sems,
    ) = refs
    places = len(cache_refs) // 2
    sources, slots = out_ref.shape[0], out_ref.shape[2]
    rows, width = held.shape[1], held.shape[2]
    heads = width // HEAD
    parts = rows // 8
    scale = math.log2(math.e) / math.sqrt(HEAD)

    loads = []
    for place in range(places):
        for side, (whole, cached) in enumerate(
            ((keys, cache_refs[place]), (values, cache_refs[places + place]))
        ):
            loads.append(
                pltpu.make_async_copy(
                    cached, whole.at[pl.ds(place * CAPC, CAPC)], cache_sems.at[2 * place + side]
                )
            )
            loads[-1].start()

    def collect(index, found):
        slot = index // sources
        source = index - slot * sources
        row = tags_ref[source, first_slot + slot]

        @pl.when(row > 0)
        def _():
            pltpu.make_async_copy(
                sent_ref.at[
                    source, pl.ds(pl.multiple_of((slot + sent_slot) * rows, rows), rows)
                ],
                held.at[found],
                in_sems.at[found],
            ).start()
            at_ref[found] = index
            cache_ref[found] = slot // CAPC * CAPC + row - 1
            length_ref[found] = tags_ref[source, 64 + first_slot + slot]

        return found + jnp.where(row > 0, 1, 0)

    found = lax.fori_loop(0, sources * slots, collect, 0)
    for spare in range(2):
        cache_ref[found + spare] = 0
        length_ref[found + spare] = 0
    for load in loads:
        load.wait()

    def arrive(index, carry):
        pltpu.make_async_copy(sent_ref.at[0, pl.ds(0, rows)], held.at[index], in_sems.at[index]).wait()
        return carry

    lax.fori_loop(0, found, arrive, 0)

    def score(index, scores_ref, peak_ref):
        block = jnp.concatenate(
            [held[index, :, head * HEAD : (head + 1) * HEAD] for head in range(heads)], axis=0
        )
        scores = lax.dot_general(
            block, keys[cache_ref[index]], (((1,), (1,)), ((), ())),
            preferred_element_type=jnp.float32,
        )
        scores_ref[...] = scores
        peak_ref[...] = jnp.broadcast_to(jnp.max(scores, axis=1, keepdims=True), peak_ref.shape)

    def mix(index, scores_ref, peak_ref):
        peak = peak_ref[:, :1]
        weights = jnp.exp2((scores_ref[...] - peak) * scale)
        total = jnp.sum(weights, axis=1, keepdims=True)
        mixed = lax.dot_general(
            weights.astype(jnp.bfloat16), values[cache_ref[index]], (((1,), (0,)), ((), ())),
            preferred_element_type=jnp.float32,
        )
        mixed = mixed * (1.0 / total)
        line = lax.broadcasted_iota(jnp.int32, (8, HEAD), 0)
        length = length_ref[index]
        for part in range(parts):
            live = line + 8 * part < length
            for head in range(heads):
                piece = mixed[head * rows + 8 * part : head * rows + 8 * part + 8]
                staged[index, part, :, head * HEAD : (head + 1) * HEAD] = jnp.where(
                    live, piece, 0.0
                ).astype(jnp.bfloat16)

    def deliver(index):
        at = at_ref[index]
        slot = at // sources
        pltpu.make_async_copy(
            staged.at[index], out_ref.at[at - slot * sources, :, slot], out_sems.at[index]
        ).start()

    score(0, even_scores, even_peak)

    def pair(step, carry):
        first = 2 * step
        score(first + 1, odd_scores, odd_peak)
        mix(first, even_scores, even_peak)
        deliver(first)
        score(first + 2, even_scores, even_peak)
        mix(first + 1, odd_scores, odd_peak)

        @pl.when(first + 1 < found)
        def _():
            deliver(first + 1)

        return carry

    lax.fori_loop(0, (found + 1) // 2, pair, 0)

    def leave(index, carry):
        pltpu.make_async_copy(staged.at[index], out_ref.at[0, :, 0], out_sems.at[index]).wait()
        return carry

    lax.fori_loop(0, found, leave, 0)


def join_kernel(bounds, z_ref, slots_ref, prompts_ref, *refs):
    count = len(bounds) - 1
    moved_refs = refs[:count]
    out_ref, held, slot_ref, prompt_ref, counts_ref, item_ref, in_sems, out_sems, sems = refs[-9:]
    items = held.shape[0]
    columns, width = moved_refs[0].shape[1], moved_refs[0].shape[4]
    smalls = [
        pltpu.make_async_copy(slots_ref, slot_ref, sems.at[0]),
        pltpu.make_async_copy(prompts_ref, prompt_ref, sems.at[1]),
    ]
    for copy in smalls:
        copy.start()
    my_z = z_ref[0]
    for group in range(counts_ref.shape[0]):
        counts_ref[group] = 0
    for copy in smalls:
        copy.wait()

    def fetch(item, found):
        owner_x, slot, _ = route(prompt_ref[item], slot_ref, counts_ref, my_z)
        for index in range(count):
            low, high = bounds[index], bounds[index + 1]

            @pl.when((slot >= low) & (slot < high))
            def _(index=index, low=low):
                for column in range(columns):
                    pltpu.make_async_copy(
                        moved_refs[index].at[owner_x, column, slot - low],
                        held.at[found, :, pl.ds(column * width, width)],
                        in_sems.at[found],
                    ).start()
                item_ref[found] = item

        inside = (slot >= bounds[0]) & (slot < bounds[-1])
        return found + jnp.where(inside, 1, 0)

    found = lax.fori_loop(0, items, fetch, 0)

    def place(index, carry):
        pltpu.make_async_copy(out_ref.at[0], held.at[index], in_sems.at[index]).wait()
        pltpu.make_async_copy(
            held.at[index], out_ref.at[item_ref[index]], out_sems.at[index]
        ).start()
        return carry

    lax.fori_loop(0, found, place, 0)

    def leave(index, carry):
        pltpu.make_async_copy(held.at[index], out_ref.at[0], out_sems.at[index]).wait()
        return carry

    lax.fori_loop(0, found, leave, 0)


def smem():
    return pl.BlockSpec(memory_space=pltpu.SMEM)


def hbm():
    return pl.BlockSpec(memory_space=pltpu.HBM)


def attend_call(tags, sent, used, first, count, ts=8, sent_slot=0, after=None):
    xs, rows, width = sent.shape[0], 64, sent.shape[2]
    heads, prefix = width // HEAD, used[0][0].shape[1]
    return pl.pallas_call(
        functools.partial(attend_kernel, first, sent_slot),
        out_shape=jax.ShapeDtypeStruct((xs, ts, count, rows // ts, width), jnp.bfloat16),
        in_specs=[smem(), hbm(), hbm()] + [hbm()] * (2 * len(used)),
        out_specs=hbm(),
        scratch_shapes=[
            pltpu.VMEM((xs * count + 2, rows, width), jnp.bfloat16),
            pltpu.VMEM((xs * count + 1, ts, rows // ts, width), jnp.bfloat16),
            pltpu.VMEM((count, prefix, HEAD), jnp.bfloat16),
            pltpu.VMEM((count, prefix, HEAD), jnp.bfloat16),
            pltpu.VMEM((rows * heads, prefix), jnp.float32),
            pltpu.VMEM((rows * heads, prefix), jnp.float32),
            pltpu.VMEM((rows * heads, HEAD), jnp.float32),
            pltpu.VMEM((rows * heads, HEAD), jnp.float32),
            pltpu.SMEM((xs * count + 2,), jnp.int32),
            pltpu.SMEM((xs * count + 2,), jnp.int32),
            pltpu.SMEM((xs * count + 2,), jnp.int32),
            pltpu.SemaphoreType.DMA((xs * count,)),
            pltpu.SemaphoreType.DMA((xs * count,)),
            pltpu.SemaphoreType.DMA((count,)),
        ],
        compiler_params=pltpu.CompilerParams(vmem_limit_bytes=VMEM),
        cost_estimate=pl.CostEstimate(
            flops=4 * xs * count * rows * heads * prefix * HEAD,
            bytes_accessed=4 * xs * count * rows * width,
            transcendentals=xs * count * rows * heads * prefix,
        ),
    )(tags, sent, tags if after is None else after, *[c[0] for c in used], *[c[1] for c in used])


def steps(queries, prefix_keys, prefix_values, slot_of_prompt, prompt_of, lengths):
    xs, zs, ts = lax.axis_size("x"), lax.axis_size("z"), lax.axis_size("t")
    items, rows, width = queries.shape
    prefix = prefix_keys.shape[1]
    my_z = lax.axis_index("z").reshape(1)
    slot_total = zs * CAPC
    near_slots = NEAR * CAPC
    far_slots = slot_total - near_slots

    up = [(i, (i + 1) % zs) for i in range(zs)]
    down = [(i, (i - 1) % zs) for i in range(zs)]
    from_below, from_above = [(prefix_keys, prefix_values)], [(prefix_keys, prefix_values)]
    for _ in range(1, 4):
        from_below.append(tuple(lax.ppermute(a, "z", up) for a in from_below[-1]))
        from_above.append(tuple(lax.ppermute(a, "z", down) for a in from_above[-1]))
    opposite = (lax.ppermute(from_below[3][0], "z", up), lax.ppermute(from_above[3][1], "z", down))
    caches = [from_below[0]]
    for step in range(1, 4):
        caches += [from_above[step], from_below[step]]
    caches.append(opposite)

    tables = rotary_tables(prefix, rows)

    def pack(low, high, tail):
        return pl.pallas_call(
            functools.partial(pack_kernel, low, high),
            out_shape=jax.ShapeDtypeStruct(
                (xs, (high - low) * rows + tail, width), jnp.bfloat16
            ),
            in_specs=[smem()] + [hbm()] * 5,
            out_specs=hbm(),
            scratch_shapes=[
                pltpu.VMEM((items + TURN, rows, width), jnp.bfloat16),
                pltpu.VMEM((items + TURN, rows, width), jnp.bfloat16),
                pltpu.VMEM((2, rows, HEAD), jnp.float32),
                pltpu.VMEM((xs, TAIL, HEAD), jnp.bfloat16),
                pltpu.SMEM((xs * zs * CAPC,), jnp.int32),
                pltpu.SMEM((items,), jnp.int32),
                pltpu.SMEM((items,), jnp.int32),
                pltpu.SMEM((xs * zs,), jnp.int32),
                pltpu.SMEM((items,), jnp.int32),
                pltpu.SMEM((items,), jnp.int32),
                pltpu.SemaphoreType.DMA((items,)),
                pltpu.SemaphoreType.DMA((items,)),
                pltpu.SemaphoreType.DMA((4,)),
                pltpu.SemaphoreType.DMA((xs,)),
            ],
            compiler_params=pltpu.CompilerParams(vmem_limit_bytes=VMEM),
            cost_estimate=pl.CostEstimate(
                flops=2 * 10**9, bytes_accessed=items * rows * width * 2, transcendentals=0
            ),
        )(my_z, slot_of_prompt, prompt_of, lengths, queries, tables)

    near = pack(0, near_slots, TAIL)
    far = pack(near_slots, slot_total, 0)
    near = lax.all_to_all(near, "x", 0, 0, tiled=True)
    far = lax.all_to_all(far, "x", 0, 0, tiled=True)
    tags = near[:, near_slots * rows, :].astype(jnp.int32)[:, :HEAD]

    def attend(sent, first, count, sent_slot, after):
        used = caches[first // CAPC : (first + count) // CAPC]
        return attend_call(tags, sent, used, first, count, ts, sent_slot, after)

    def back(attended):
        shape = attended.shape
        moved = lax.all_to_all(
            attended.reshape(xs * ts, *shape[2:]), ("x", "t"), 0, 0, tiled=True
        )
        return moved.reshape(shape)

    near = attend(near, 0, near_slots, 0, None)
    far = attend(far, near_slots, far_slots, 0, near)
    near = back(near)
    far = back(far)

    def join(bounds, moved, out):
        more = [] if out is None else [out]
        return pl.pallas_call(
            functools.partial(join_kernel, bounds),
            out_shape=jax.ShapeDtypeStruct((items, rows // ts, width * ts), jnp.bfloat16),
            in_specs=[smem()] + [hbm()] * (2 + len(moved) + len(more)),
            out_specs=hbm(),
            input_output_aliases={3 + len(moved): 0} if more else {},
            scratch_shapes=[
                pltpu.VMEM((items, rows // ts, width * ts), jnp.bfloat16),
                pltpu.SMEM((xs * zs * CAPC,), jnp.int32),
                pltpu.SMEM((items,), jnp.int32),
                pltpu.SMEM((xs * zs,), jnp.int32),
                pltpu.SMEM((items,), jnp.int32),
                pltpu.SemaphoreType.DMA((items,)),
                pltpu.SemaphoreType.DMA((items,)),
                pltpu.SemaphoreType.DMA((2,)),
            ],
            compiler_params=pltpu.CompilerParams(vmem_limit_bytes=VMEM),
            cost_estimate=pl.CostEstimate(
                flops=10**9, bytes_accessed=2 * items * rows * width, transcendentals=0
            ),
        )(my_z, slot_of_prompt, prompt_of, *moved, *more)

    out = join((0, near_slots), [near], None)
    return join((near_slots, slot_total), [far], out)


def solution(mesh):
    groups, tensors = mesh.devices.shape
    grid = Mesh(
        mesh.devices.reshape(groups // GROUPS_Z, GROUPS_Z, tensors), ("x", "z", "t")
    )
    split = P(("x", "z"), None, "t")
    return jax.shard_map(
        steps,
        mesh=grid,
        in_specs=(split, split, split, P(), P(("x", "z")), P(("x", "z"))),
        out_specs=P(("x", "z"), "t", None),
        check_vma=False,
    )
```

time: 397 us -> 204 us (0.51)
  local copies, waits for them, and re-layouts: 86.6 us -> 2.45 us
  waiting for transfers between devices: 151 us -> 96.1 us
  matrix products: 53.5 us -> 0 us
  Pallas kernels: 0 us -> 45.5 us
  other arithmetic: 41.2 us -> 0.59 us
  starting transfers between devices: 62.8 us -> 57.9 us
    all_to_all x7 -> x4, waiting for transfers between devices: 151 us -> 47.4 us  [the longest x1 24.6 us: steps(): near = lax.all_to_all(near, 'x', 0, 0, tiled=True)]
    dot_general x32 -> x0, matrix products: 53.5 us -> none  [the longest x8 21.4 us: attend_block(): jnp.einsum('bkgrp,bpkd->brkgd', probabilities, value_heads, preferred_ele...]
    ppermute x0 -> x14, waiting for transfers between devices: none -> 48.7 us  [the longest x6 23.4 us: steps(): from_below.append(tuple((lax.ppermute(a, 'z', up) for a in from_below[-1])))]
    pallas_call x0 -> x6, Pallas kernels: none -> 45.5 us  [the longest x2 28.7 us: attend_call(): pl.pallas_call(functools.partial(attend_kernel, first, sent_slot), out_sh...]
    all_to_all x7 -> x4, starting transfers between devices: 62.8 us -> 30.1 us  [the longest x2 20.9 us: back(): lax.all_to_all(attended.reshape(xs * ts, *shape[2:]), ('x', 't'), 0, 0, t...]
    ppermute x0 -> x14, starting transfers between devices: none -> 27.8 us  [the longest x6 24.5 us: steps(): lax.ppermute(a, 'z', down)]
    another operation x10 -> x0, local copies, waits for them, and re-layouts: 18.1 us -> none
    reduce_sum x10 -> x0, other arithmetic: 16.3 us -> none  [the longest x8 16 us: attend_block(): denominator = jnp.sum(weights, axis=-1)]
  transfers between devices with their start and end apart: 7 -> 18, of which waited for: 4 -> 9; matrix products, arithmetic and copies ran while one was open for 41% -> 1% of each run, Pallas kernels for 0% -> 18%
where the time goes in v1:
time: 204 us; the launch traced here: 203 us
  waiting for transfers between devices  96.1 us (47%)
  starting transfers between devices  57.9 us (28%)
  Pallas kernels  45.5 us (22%)
  local copies, waits for them, and re-layouts  2.45 us (1%)
    pallas_call x2, Pallas kernels, attend_call(): pl.pallas_call(functools.partial(attend_kernel, first, sent_slot), out_sh...  28.7 us
    all_to_all x1, waiting for transfers between devices, steps(): near = lax.all_to_all(near, 'x', 0, 0, tiled=True)  24.6 us
    ppermute x6, starting transfers between devices, steps(): lax.ppermute(a, 'z', down)  24.5 us
    ppermute x6, waiting for transfers between devices, steps(): from_below.append(tuple((lax.ppermute(a, 'z', up) for a in from_below[-1])))  23.4 us
    all_to_all x2, waiting for transfers between devices, back(): lax.all_to_all(attended.reshape(xs * ts, *shape[2:]), ('x', 't'), 0, 0, t...  22.8 us
    all_to_all x2, starting transfers between devices, back(): lax.all_to_all(attended.reshape(xs * ts, *shape[2:]), ('x', 't'), 0, 0, t...  20.9 us
    ppermute x6, waiting for transfers between devices, steps(): lax.ppermute(a, 'z', down)  14.1 us
    ppermute x1, waiting for transfers between devices, steps(): lax.ppermute(from_below[3][0], 'z', up)  11.2 us
  transfers between devices with their start and end apart: 18, of which 9 were waited for; matrix products, arithmetic and copies ran while one was open for 1% of the time, Pallas kernels for 18%

profile of v1, /device:TPU:1, one launch (start us, length us, event | category | flops | bytes accessed | tf_op | source)
XLA Modules:
  0.0 202.7 jit_solution(15169058528975770980)
XLA Ops:
  0.0 4.5 %shard_map.73 = bf16[4,656,640]{2,1,0:T(8,128)(2,1)} custom-call(s32[1]{0:T(128)} %bitcast.z_ref, s32[64]{0:T(128)} %slots_ref.7, s32[32]{0:T(128)} %prompts_ref.7, s32[32]{0:T(128)} %lengths_ref.3, bf16[32,64,640]{2,1,0:T(8,128)(2,1)} %queries_ref.3, f32[2,64,128]{2,1,0:T(8,128)} %constant.7.clone.tables_ref), custom_call_target="tpu_custom_call" | custom-call | flops 2000000000 | bytes 2621440 | tf_op jit(solution)/shard_map/pallas_call | solution.py:387
  4.5 4.7 %all-to-all-start = ((bf16[4,656,640]{2,1,0:T(8,128)(2,1)}), bf16[4,656,640]{2,1,0:T(8,128)(2,1)}, u32[]{:S(2)}, u32[]{:S(2)}) async-start(bf16[4,656,640]{2,1,0:T(8,128)(2,1)} %shard_map.73), calls=%async_computation | async-start | bytes 6717440 | tf_op jit(solution)/shard_map/all_to_all | solution.py:418
  9.2 6.4 %collective-permute-start = (bf16[2,1024,128]{2,1,0:T(8,128)(2,1)}, bf16[2,1024,128]{2,1,0:T(8,128)(2,1)}, u32[]{:S(2)}, u32[]{:S(2)}) collective-permute-start(bf16[2,1024,128]{2,1,0:T(8,128)(2,1)} %refs_0_.1), channel_id=1, source_target_pairs={{0,56},{8,0},{16,8},{24,16},{32,24},{40,32},{48,40},{56,48},{1,57}... | collective-permute-start | bytes 1572872 | tf_op jit(solution)/shard_map/ppermute | solution.py:377
  15.6 0.0 collective-permute-start.1
  15.6 2.7 %collective-permute-start.4 = (bf16[2,1024,128]{2,1,0:T(8,128)(2,1)}, bf16[2,1024,128]{2,1,0:T(8,128)(2,1)}, u32[]{:S(2)}, u32[]{:S(2)}) collective-permute-start(bf16[2,1024,128]{2,1,0:T(8,128)(2,1)} %refs_5_.1), channel_id=1, source_target_pairs={{0,56},{8,0},{16,8},{24,16},{32,24},{40,32},{48,40},{56,48},{1,57}... | collective-permute-start | bytes 1572872 | tf_op jit(solution)/shard_map/ppermute | solution.py:377
  18.3 0.0 collective-permute-start.5
  18.3 4.1 %shard_map.74 = bf16[4,384,640]{2,1,0:T(8,128)(2,1)} custom-call(s32[1]{0:T(128)} %bitcast.z_ref, s32[64]{0:T(128)} %slots_ref.7, s32[32]{0:T(128)} %prompts_ref.7, s32[32]{0:T(128)} %lengths_ref.3, bf16[32,64,640]{2,1,0:T(8,128)(2,1)} %queries_ref.3, f32[2,64,128]{2,1,0:T(8,128)} %constant.7.clone.tables_ref), custom_call_target="tpu_custom_call" | custom-call | flops 2000000000 | bytes 2621440 | tf_op jit(solution)/shard_map/pallas_call | solution.py:387
  22.4 24.6 %all-to-all-done.sent_ref = bf16[4,656,640]{2,1,0:T(8,128)(2,1)} async-done(((bf16[4,656,640]{2,1,0:T(8,128)(2,1)}), bf16[4,656,640]{2,1,0:T(8,128)(2,1)}, u32[]{:S(2)}, u32[]{:S(2)}) %all-to-all-start) | async-done | bytes 3358752 | tf_op jit(solution)/shard_map/all_to_all | solution.py:418
  47.0 4.4 %all-to-all-start.1 = ((bf16[4,384,640]{2,1,0:T(8,128)(2,1)}), bf16[4,384,640]{2,1,0:T(8,128)(2,1)}, u32[]{:S(2)}, u32[]{:S(2)}) async-start(bf16[4,384,640]{2,1,0:T(8,128)(2,1)} %shard_map.74), calls=%async_computation.1 | async-start | bytes 3932160 | tf_op jit(solution)/shard_map/all_to_all | solution.py:419
  51.4 0.0 collective-permute-done.refs_1_
  51.4 8.0 %collective-permute-start.2 = (bf16[2,1024,128]{2,1,0:T(8,128)(2,1)}, bf16[2,1024,128]{2,1,0:T(8,128)(2,1)}, u32[]{:S(2)}, u32[]{:S(2)}) collective-permute-start(bf16[2,1024,128]{2,1,0:T(8,128)(2,1)} %collective-permute-done.refs_1_), channel_id=1, source_target_pairs={{0,56},{8,0},{16,8},{24,16},{32,24},{40,32},{48,40},{56,48},{1,57}... | collective-permute-start | bytes 1572872 | tf_op jit(solution)/shard_map/ppermute | solution.py:377
  59.4 0.0 collective-permute-done.1.refs_2_
  59.4 0.0 collective-permute-start.3
  59.4 0.0 collective-permute-done.4.refs_6_
  59.4 2.7 %collective-permute-start.6 = (bf16[2,1024,128]{2,1,0:T(8,128)(2,1)}, bf16[2,1024,128]{2,1,0:T(8,128)(2,1)}, u32[]{:S(2)}, u32[]{:S(2)}) collective-permute-start(bf16[2,1024,128]{2,1,0:T(8,128)(2,1)} %collective-permute-done.4.refs_6_), channel_id=1, source_target_pairs={{0,56},{8,0},{16,8},{24,16},{32,24},{40,32},{48,40},{56,48},{1,57}... | collective-permute-start | bytes 1572872 | tf_op jit(solution)/shard_map/ppermute | solution.py:377
  62.0 0.0 collective-permute-done.5.refs_7_
  62.1 0.0 collective-permute-start.7
  62.1 0.8 slice.11
  62.9 0.6 slice_convert_fusion.tags_ref.after_ref
  63.4 6.0 %collective-permute-done.2.refs_3_ = bf16[2,1024,128]{2,1,0:T(8,128)(2,1)} collective-permute-done((bf16[2,1024,128]{2,1,0:T(8,128)(2,1)}, bf16[2,1024,128]{2,1,0:T(8,128)(2,1)}, u32[]{:S(2)}, u32[]{:S(2)}) %collective-permute-start.2) | collective-permute-done | bytes 524320 | tf_op jit(solution)/shard_map/ppermute | solution.py:377
  69.4 3.1 %collective-permute-done.3.refs_4_ = bf16[2,1024,128]{2,1,0:T(8,128)(2,1)} collective-permute-done((bf16[2,1024,128]{2,1,0:T(8,128)(2,1)}, bf16[2,1024,128]{2,1,0:T(8,128)(2,1)}, u32[]{:S(2)}, u32[]{:S(2)}) %collective-permute-start.3) | collective-permute-done | bytes 524320 | tf_op jit(solution)/shard_map/ppermute | solution.py:376
  72.6 8.1 %collective-permute-done.6.refs_8_ = bf16[2,1024,128]{2,1,0:T(8,128)(2,1)} collective-permute-done((bf16[2,1024,128]{2,1,0:T(8,128)(2,1)}, bf16[2,1024,128]{2,1,0:T(8,128)(2,1)}, u32[]{:S(2)}, u32[]{:S(2)}) %collective-permute-start.6) | collective-permute-done | bytes 524320 | tf_op jit(solution)/shard_map/ppermute | solution.py:377
  80.7 3.1 %collective-permute-done.7.refs_9_ = bf16[2,1024,128]{2,1,0:T(8,128)(2,1)} collective-permute-done((bf16[2,1024,128]{2,1,0:T(8,128)(2,1)}, bf16[2,1024,128]{2,1,0:T(8,128)(2,1)}, u32[]{:S(2)}, u32[]{:S(2)}) %collective-permute-start.7) | collective-permute-done | bytes 524320 | tf_op jit(solution)/shard_map/ppermute | solution.py:376
  83.8 18.4 %shard_map.75.after_ref = bf16[4,8,10,8,640]{4,3,2,1,0:T(8,128)(2,1)} custom-call(s32[4,128]{1,0:T(4,128)} %slice_convert_fusion.tags_ref.after_ref, bf16[4,656,640]{2,1,0:T(8,128)(2,1)} %all-to-all-done.sent_ref, s32[4,128]{1,0:T(4,128)} %slice_convert_fusion.tags_ref.after_ref, bf16[2,1024,128]{2,1,0:T(8,128)(2,1)} %refs_0_.1, ...), custom_call_target="tpu_custom_call" | custom-call | flops 6710886400 | bytes 6553600 | tf_op jit(solution)/shard_map/pallas_call | solution.py:333
  102.2 0.0 all-to-all-done.1.sent_ref
  102.2 9.6 %all-to-all-start.3 = ((bf16[32,10,8,640]{3,2,1,0:T(8,128)(2,1)}), bf16[32,10,8,640]{3,2,1,0:T(8,128)(2,1)}, u32[]{:S(2)}, u32[]{:S(2)}) async-start(bf16[32,10,8,640]{3,2,1,0:T(8,128)(2,1)} %bitcast.8), calls=%async_computation.3 | async-start | bytes 6553600 | tf_op jit(solution)/shard_map/all_to_all | solution.py:428
  111.9 0.6 collective-permute-start.9
  112.5 2.2 %collective-permute-start.11 = (bf16[2,1024,128]{2,1,0:T(8,128)(2,1)}, bf16[2,1024,128]{2,1,0:T(8,128)(2,1)S(1)}, u32[]{:S(2)}, u32[]{:S(2)}) collective-permute-start(bf16[2,1024,128]{2,1,0:T(8,128)(2,1)} %collective-permute-done.6.refs_8_), channel_id=1, source_target_pairs={{0,56},{8,0},{16,8},{24,16},{32,24},{40,32},{48,40},{56,48},{1,57}... | collective-permute-start | bytes 1572872 | tf_op jit(solution)/shard_map/ppermute | solution.py:377
  114.6 0.0 collective-permute-start.12
  114.6 2.7 %collective-permute-start.8 = (bf16[2,1024,128]{2,1,0:T(8,128)(2,1)}, bf16[2,1024,128]{2,1,0:T(8,128)(2,1)S(1)}, u32[]{:S(2)}, u32[]{:S(2)}) collective-permute-start(bf16[2,1024,128]{2,1,0:T(8,128)(2,1)} %collective-permute-done.2.refs_3_), channel_id=1, source_target_pairs={{0,56},{8,0},{16,8},{24,16},{32,24},{40,32},{48,40},{56,48},{1,57}... | collective-permute-start | bytes 1572872 | tf_op jit(solution)/shard_map/ppermute | solution.py:377
  117.3 9.4 %collective-permute-done.9.refs_1_ = bf16[2,1024,128]{2,1,0:T(8,128)(2,1)S(1)} collective-permute-done((bf16[2,1024,128]{2,1,0:T(8,128)(2,1)}, bf16[2,1024,128]{2,1,0:T(8,128)(2,1)S(1)}, u32[]{:S(2)}, u32[]{:S(2)}) %collective-permute-start.9) | collective-permute-done | bytes 524320 | tf_op jit(solution)/shard_map/ppermute | solution.py:376
  126.7 0.8 copy-done
  127.5 0.0 collective-permute-start.10
  127.5 0.0 collective-permute-done.11.refs_3_
  127.5 2.7 %collective-permute-start.13 = (bf16[2,1024,128]{2,1,0:T(8,128)(2,1)S(1)}, bf16[2,1024,128]{2,1,0:T(8,128)(2,1)}, u32[]{:S(2)}, u32[]{:S(2)}) collective-permute-start(bf16[2,1024,128]{2,1,0:T(8,128)(2,1)S(1)} %collective-permute-done.11.refs_3_), channel_id=1, source_target_pairs={{0,56},{8,0},{16,8},{24,16},{32,24},{40,32},{48,40},{56,48},{1,57}... | collective-permute-start | bytes 1572872 | tf_op jit(solution)/shard_map/ppermute | solution.py:378
  130.1 7.7 %collective-permute-done.12.refs_4_ = bf16[2,1024,128]{2,1,0:T(8,128)(2,1)S(1)} collective-permute-done((bf16[2,1024,128]{2,1,0:T(8,128)(2,1)}, bf16[2,1024,128]{2,1,0:T(8,128)(2,1)S(1)}, u32[]{:S(2)}, u32[]{:S(2)}) %collective-permute-start.12) | collective-permute-done | bytes 524320 | tf_op jit(solution)/shard_map/ppermute | solution.py:376
  137.9 0.0 collective-permute-done.8.refs_0_
  137.9 11.2 %collective-permute-done.10.refs_2_ = bf16[2,1024,128]{2,1,0:T(8,128)(2,1)S(1)} collective-permute-done((bf16[2,1024,128]{2,1,0:T(8,128)(2,1)S(1)}, bf16[2,1024,128]{2,1,0:T(8,128)(2,1)S(1)}, u32[]{:S(2)}, u32[]{:S(2)}) %collective-permute-start.10) | collective-permute-done | bytes 524320 | tf_op jit(solution)/shard_map/ppermute | solution.py:378
  149.1 0.0 copy-done.1
  149.1 0.0 copy-start.4
  149.1 0.8 copy-done.4
  150.0 0.0 collective-permute-done.13.refs_5_
  150.0 10.3 %shard_map.76 = bf16[4,8,6,8,640]{4,3,2,1,0:T(8,128)(2,1)} custom-call(s32[4,128]{1,0:T(4,128)} %slice_convert_fusion.tags_ref.after_ref, bf16[4,384,640]{2,1,0:T(8,128)(2,1)} %all-to-all-done.1.sent_ref, bf16[4,8,10,8,640]{4,3,2,1,0:T(8,128)(2,1)} %shard_map.75.after_ref, bf16[2,1024,128]{2,1,0:T(8,128)(2,1)} %copy-done.3, bf16[2,1024,128]{2,1,0:T(8,128)(2,1)} %copy-done, ...), custom_call_target="tpu_custom_call" | custom-call | flops 4026531840 | bytes 3932160 | tf_op jit(solution)/shard_map/pallas_call | solution.py:333
  160.3 0.0 all-to-all-done.3
  160.3 11.3 %all-to-all-start.2 = ((bf16[32,6,8,640]{3,2,1,0:T(8,128)(2,1)}), bf16[32,6,8,640]{3,2,1,0:T(8,128)(2,1)}, u32[]{:S(2)}, u32[]{:S(2)}) async-start(bf16[32,6,8,640]{3,2,1,0:T(8,128)(2,1)} %bitcast.9), calls=%async_computation.2 | async-start | bytes 3932160 | tf_op jit(solution)/shard_map/all_to_all | solution.py:428
  171.6 4.2 %shard_map.77.refs_1_ = bf16[32,8,5120]{2,1,0:T(8,128)(2,1)} custom-call(s32[1]{0:T(128)} %bitcast.z_ref, s32[64]{0:T(128)} %slots_ref.7, s32[32]{0:T(128)} %prompts_ref.7, bf16[4,8,10,8,640]{4,3,2,1,0:T(8,128)(2,1)} %bitcast.5.refs_0_), custom_call_target="tpu_custom_call" | custom-call | flops 1000000000 | bytes 2621440 | tf_op jit(solution)/shard_map/pallas_call | solution.py:440
  175.8 22.8 %all-to-all-done.2 = bf16[32,6,8,640]{3,2,1,0:T(8,128)(2,1)} async-done(((bf16[32,6,8,640]{3,2,1,0:T(8,128)(2,1)}), bf16[32,6,8,640]{3,2,1,0:T(8,128)(2,1)}, u32[]{:S(2)}, u32[]{:S(2)}) %all-to-all-start.2) | async-done | bytes 1966112 | tf_op jit(solution)/shard_map/all_to_all | solution.py:428
  198.6 3.9 %shard_map.78 = bf16[32,8,5120]{2,1,0:T(8,128)(2,1)} custom-call(s32[1]{0:T(128)} %bitcast.z_ref, s32[64]{0:T(128)} %slots_ref.7, s32[32]{0:T(128)} %prompts_ref.7, bf16[4,8,6,8,640]{4,3,2,1,0:T(8,128)(2,1)} %bitcast.3.refs_0_, bf16[32,8,5120]{2,1,0:T(8,128)(2,1)} %shard_map.77.refs_1_), custom_call_target="tpu_custom_call", output_to_operand_aliasing={{}: (4, {})} | custom-call | flops 1000000000 | bytes 2621440 | tf_op jit(solution)/shard_map/pallas_call | solution.py:440
  (7 shorter events, 0.0 us)
Async XLA Ops:
  4.5 42.5 %all-to-all-start = ((bf16[4,656,640]{2,1,0:T(8,128)(2,1)}), bf16[4,656,640]{2,1,0:T(8,128)(2,1)}, u32[]{:S(2)}, u32[]{:S(2)}) async-start(bf16[4,656,640]{2,1,0:T(8,128)(2,1)} %shard_map.73), calls=%async_computation | async-start | bytes 6717440 | tf_op jit(solution)/shard_map/all_to_all | solution.py:418
  9.2 42.2 %collective-permute-start = (bf16[2,1024,128]{2,1,0:T(8,128)(2,1)}, bf16[2,1024,128]{2,1,0:T(8,128)(2,1)}, u32[]{:S(2)}, u32[]{:S(2)}) collective-permute-start(bf16[2,1024,128]{2,1,0:T(8,128)(2,1)} %refs_0_.1), channel_id=1, source_target_pairs={{0,56},{8,0},{16,8},{24,16},{32,24},{40,32},{48,40},{56,48},{1,57}... | collective-permute-start | bytes 1572872 | tf_op jit(solution)/shard_map/ppermute | solution.py:377
  15.6 43.8 %collective-permute-start.1 = (bf16[2,1024,128]{2,1,0:T(8,128)(2,1)}, bf16[2,1024,128]{2,1,0:T(8,128)(2,1)}, u32[]{:S(2)}, u32[]{:S(2)}) collective-permute-start(bf16[2,1024,128]{2,1,0:T(8,128)(2,1)} %refs_0_.1), channel_id=1, source_target_pairs={{0,8},{8,16},{16,24},{24,32},{32,40},{40,48},{48,56},{56,0},{1,9},... | collective-permute-start | bytes 1572872 | tf_op jit(solution)/shard_map/ppermute | solution.py:376
  15.6 43.8 %collective-permute-start.4 = (bf16[2,1024,128]{2,1,0:T(8,128)(2,1)}, bf16[2,1024,128]{2,1,0:T(8,128)(2,1)}, u32[]{:S(2)}, u32[]{:S(2)}) collective-permute-start(bf16[2,1024,128]{2,1,0:T(8,128)(2,1)} %refs_5_.1), channel_id=1, source_target_pairs={{0,56},{8,0},{16,8},{24,16},{32,24},{40,32},{48,40},{56,48},{1,57}... | collective-permute-start | bytes 1572872 | tf_op jit(solution)/shard_map/ppermute | solution.py:377
  18.3 43.8 %collective-permute-start.5 = (bf16[2,1024,128]{2,1,0:T(8,128)(2,1)}, bf16[2,1024,128]{2,1,0:T(8,128)(2,1)}, u32[]{:S(2)}, u32[]{:S(2)}) collective-permute-start(bf16[2,1024,128]{2,1,0:T(8,128)(2,1)} %refs_5_.1), channel_id=1, source_target_pairs={{0,8},{8,16},{16,24},{24,32},{32,40},{40,48},{48,56},{56,0},{1,9},... | collective-permute-start | bytes 1572872 | tf_op jit(solution)/shard_map/ppermute | solution.py:376
  47.0 55.3 %all-to-all-start.1 = ((bf16[4,384,640]{2,1,0:T(8,128)(2,1)}), bf16[4,384,640]{2,1,0:T(8,128)(2,1)}, u32[]{:S(2)}, u32[]{:S(2)}) async-start(bf16[4,384,640]{2,1,0:T(8,128)(2,1)} %shard_map.74), calls=%async_computation.1 | async-start | bytes 3932160 | tf_op jit(solution)/shard_map/all_to_all | solution.py:419
  51.4 18.0 %collective-permute-start.2 = (bf16[2,1024,128]{2,1,0:T(8,128)(2,1)}, bf16[2,1024,128]{2,1,0:T(8,128)(2,1)}, u32[]{:S(2)}, u32[]{:S(2)}) collective-permute-start(bf16[2,1024,128]{2,1,0:T(8,128)(2,1)} %collective-permute-done.refs_1_), channel_id=1, source_target_pairs={{0,56},{8,0},{16,8},{24,16},{32,24},{40,32},{48,40},{56,48},{1,57}... | collective-permute-start | bytes 1572872 | tf_op jit(solution)/shard_map/ppermute | solution.py:377
  59.4 13.2 %collective-permute-start.3 = (bf16[2,1024,128]{2,1,0:T(8,128)(2,1)}, bf16[2,1024,128]{2,1,0:T(8,128)(2,1)}, u32[]{:S(2)}, u32[]{:S(2)}) collective-permute-start(bf16[2,1024,128]{2,1,0:T(8,128)(2,1)} %collective-permute-done.1.refs_2_), channel_id=1, source_target_pairs={{0,8},{8,16},{16,24},{24,32},{32,40},{40,48},{48,56},{56,0},{1,9},... | collective-permute-start | bytes 1572872 | tf_op jit(solution)/shard_map/ppermute | solution.py:376
  59.4 21.3 %collective-permute-start.6 = (bf16[2,1024,128]{2,1,0:T(8,128)(2,1)}, bf16[2,1024,128]{2,1,0:T(8,128)(2,1)}, u32[]{:S(2)}, u32[]{:S(2)}) collective-permute-start(bf16[2,1024,128]{2,1,0:T(8,128)(2,1)} %collective-permute-done.4.refs_6_), channel_id=1, source_target_pairs={{0,56},{8,0},{16,8},{24,16},{32,24},{40,32},{48,40},{56,48},{1,57}... | collective-permute-start | bytes 1572872 | tf_op jit(solution)/shard_map/ppermute | solution.py:377
  62.1 21.8 %collective-permute-start.7 = (bf16[2,1024,128]{2,1,0:T(8,128)(2,1)}, bf16[2,1024,128]{2,1,0:T(8,128)(2,1)}, u32[]{:S(2)}, u32[]{:S(2)}) collective-permute-start(bf16[2,1024,128]{2,1,0:T(8,128)(2,1)} %collective-permute-done.5.refs_7_), channel_id=1, source_target_pairs={{0,8},{8,16},{16,24},{24,32},{32,40},{40,48},{48,56},{56,0},{1,9},... | collective-permute-start | bytes 1572872 | tf_op jit(solution)/shard_map/ppermute | solution.py:376
  102.2 58.1 %all-to-all-start.3 = ((bf16[32,10,8,640]{3,2,1,0:T(8,128)(2,1)}), bf16[32,10,8,640]{3,2,1,0:T(8,128)(2,1)}, u32[]{:S(2)}, u32[]{:S(2)}) async-start(bf16[32,10,8,640]{3,2,1,0:T(8,128)(2,1)} %bitcast.8), calls=%async_computation.3 | async-start | bytes 6553600 | tf_op jit(solution)/shard_map/all_to_all | solution.py:428
  111.9 14.8 %collective-permute-start.9 = (bf16[2,1024,128]{2,1,0:T(8,128)(2,1)}, bf16[2,1024,128]{2,1,0:T(8,128)(2,1)S(1)}, u32[]{:S(2)}, u32[]{:S(2)}) collective-permute-start(bf16[2,1024,128]{2,1,0:T(8,128)(2,1)} %collective-permute-done.3.refs_4_), channel_id=1, source_target_pairs={{0,8},{8,16},{16,24},{24,32},{32,40},{40,48},{48,56},{56,0},{1,9},... | collective-permute-start | bytes 1572872 | tf_op jit(solution)/shard_map/ppermute | solution.py:376
  112.5 15.0 %collective-permute-start.11 = (bf16[2,1024,128]{2,1,0:T(8,128)(2,1)}, bf16[2,1024,128]{2,1,0:T(8,128)(2,1)S(1)}, u32[]{:S(2)}, u32[]{:S(2)}) collective-permute-start(bf16[2,1024,128]{2,1,0:T(8,128)(2,1)} %collective-permute-done.6.refs_8_), channel_id=1, source_target_pairs={{0,56},{8,0},{16,8},{24,16},{32,24},{40,32},{48,40},{56,48},{1,57}... | collective-permute-start | bytes 1572872 | tf_op jit(solution)/shard_map/ppermute | solution.py:377
  114.6 23.3 %collective-permute-start.12 = (bf16[2,1024,128]{2,1,0:T(8,128)(2,1)}, bf16[2,1024,128]{2,1,0:T(8,128)(2,1)S(1)}, u32[]{:S(2)}, u32[]{:S(2)}) collective-permute-start(bf16[2,1024,128]{2,1,0:T(8,128)(2,1)} %collective-permute-done.7.refs_9_), channel_id=1, source_target_pairs={{0,8},{8,16},{16,24},{24,32},{32,40},{40,48},{48,56},{56,0},{1,9},... | collective-permute-start | bytes 1572872 | tf_op jit(solution)/shard_map/ppermute | solution.py:376
  114.6 23.3 %collective-permute-start.8 = (bf16[2,1024,128]{2,1,0:T(8,128)(2,1)}, bf16[2,1024,128]{2,1,0:T(8,128)(2,1)S(1)}, u32[]{:S(2)}, u32[]{:S(2)}) collective-permute-start(bf16[2,1024,128]{2,1,0:T(8,128)(2,1)} %collective-permute-done.2.refs_3_), channel_id=1, source_target_pairs={{0,56},{8,0},{16,8},{24,16},{32,24},{40,32},{48,40},{56,48},{1,57}... | collective-permute-start | bytes 1572872 | tf_op jit(solution)/shard_map/ppermute | solution.py:377
  126.7 0.8 copy-start
  127.5 21.7 %collective-permute-start.10 = (bf16[2,1024,128]{2,1,0:T(8,128)(2,1)S(1)}, bf16[2,1024,128]{2,1,0:T(8,128)(2,1)S(1)}, u32[]{:S(2)}, u32[]{:S(2)}) collective-permute-start(bf16[2,1024,128]{2,1,0:T(8,128)(2,1)S(1)} %collective-permute-done.9.refs_1_), channel_id=1, source_target_pairs={{0,8},{8,16},{16,24},{24,32},{32,40},{40,48},{48,56},{56,0},{1,9},... | collective-permute-start | bytes 1572872 | tf_op jit(solution)/shard_map/ppermute | solution.py:378
  127.5 21.7 %copy-start.1 = (bf16[2,1024,128]{2,1,0:T(8,128)(2,1)}, bf16[2,1024,128]{2,1,0:T(8,128)(2,1)S(1)}, u32[]{:S(2)}) copy-start(bf16[2,1024,128]{2,1,0:T(8,128)(2,1)S(1)} %collective-permute-done.11.refs_3_) | copy-start | bytes 1572868
  127.5 22.5 %collective-permute-start.13 = (bf16[2,1024,128]{2,1,0:T(8,128)(2,1)S(1)}, bf16[2,1024,128]{2,1,0:T(8,128)(2,1)}, u32[]{:S(2)}, u32[]{:S(2)}) collective-permute-start(bf16[2,1024,128]{2,1,0:T(8,128)(2,1)S(1)} %collective-permute-done.11.refs_3_), channel_id=1, source_target_pairs={{0,56},{8,0},{16,8},{24,16},{32,24},{40,32},{48,40},{56,48},{1,57}... | collective-permute-start | bytes 1572872 | tf_op jit(solution)/shard_map/ppermute | solution.py:378
  137.9 11.2 %copy-start.2 = (bf16[2,1024,128]{2,1,0:T(8,128)(2,1)}, bf16[2,1024,128]{2,1,0:T(8,128)(2,1)S(1)}, u32[]{:S(2)}) copy-start(bf16[2,1024,128]{2,1,0:T(8,128)(2,1)S(1)} %collective-permute-done.12.refs_4_) | copy-start | bytes 1572868
  137.9 11.2 %copy-start.3 = (bf16[2,1024,128]{2,1,0:T(8,128)(2,1)}, bf16[2,1024,128]{2,1,0:T(8,128)(2,1)S(1)}, u32[]{:S(2)}) copy-start(bf16[2,1024,128]{2,1,0:T(8,128)(2,1)S(1)} %collective-permute-done.8.refs_0_) | copy-start | bytes 1572868
  149.1 0.8 copy-start.4
  160.3 38.3 %all-to-all-start.2 = ((bf16[32,6,8,640]{3,2,1,0:T(8,128)(2,1)}), bf16[32,6,8,640]{3,2,1,0:T(8,128)(2,1)}, u32[]{:S(2)}, u32[]{:S(2)}) async-start(bf16[32,6,8,640]{3,2,1,0:T(8,128)(2,1)} %bitcast.9), calls=%async_computation.2 | async-start | bytes 3932160 | tf_op jit(solution)/shard_map/all_to_all | solution.py:428

commit v2 on v1

--- a/solution.py
+++ b/solution.py
@@ -15,9 +15,9 @@
 ROTARY_BASE = 1000000.0
 VMEM = 67043328
 GROUPS_Z = 8
-NEAR = 5
+THERE = (0, 3 * CAPC, 8 * CAPC)
+BOUNDS = (0, 3 * CAPC, 5 * CAPC, 8 * CAPC)
 TURN = 4
-TAIL = 16
 
 
 def rotary_tables(first_position, rows):
@@ -48,13 +48,16 @@
 
 
 def pack_kernel(
-    low, high, z_ref, slots_ref, prompts_ref, lengths_ref, queries_ref, tables_ref, sent_ref,
-    held, staged, tables, tagged, slot_ref, prompt_ref, length_ref, counts_ref,
-    to_x_ref, to_slot_ref, in_sems, out_sems, small_sems, tag_sem,
+    xs, x_ref, z_ref, slots_ref, prompts_ref, lengths_ref, queries_ref, tables_ref, *refs
 ):
+    sent_refs, tag_ref = refs[:-11], refs[-11]
+    (
+        held, staged, tables, slot_ref, prompt_ref, length_ref, counts_ref,
+        in_sems, out_sems, small_sems,
+    ) = refs[-10:]
     items, rows, width = queries_ref.shape
     heads = width // HEAD
-    tagging = sent_ref.shape[1] > (high - low) * rows
+    my_x, my_z = x_ref[0], z_ref[0]
     smalls = [
         pltpu.make_async_copy(source, target, small_sems.at[index])
         for index, (source, target) in enumerate(
@@ -66,7 +69,8 @@
     ]
     for copy in smalls:
         copy.start()
-    my_z = z_ref[0]
+    for item in range(items):
+        pltpu.make_async_copy(queries_ref.at[item], held.at[item], in_sems.at[item]).start()
     for group in range(counts_ref.shape[0]):
         counts_ref[group] = 0
     line = lax.broadcasted_iota(jnp.int32, (8, HEAD), 0)
@@ -74,85 +78,51 @@
     for copy in smalls:
         copy.wait()
 
-    def plan(item, carry):
-        found, tags = carry
-        owner_x, slot, row = route(prompt_ref[item], slot_ref, counts_ref, my_z)
-        inside = (slot >= low) & (slot < high)
-
-        @pl.when(inside)
-        def _():
-            pltpu.make_async_copy(queries_ref.at[item], held.at[found], in_sems.at[found]).start()
-            to_x_ref[found] = owner_x
-            to_slot_ref[found] = slot - low
-
-        if tagging:
+    def turn(step, tags):
+        for inner in range(TURN):
+            item = step * TURN + inner
+            pltpu.make_async_copy(queries_ref.at[item], held.at[item], in_sems.at[item]).wait()
+        routes = []
+        for inner in range(TURN):
+            item = step * TURN + inner
+            owner_x, slot, row = route(prompt_ref[item], slot_ref, counts_ref, my_z)
+            routes.append((item, lax.rem(owner_x - my_x + xs, xs), slot))
             tags = jnp.where((line == owner_x) & (lane == slot), row + 1, tags)
             tags = jnp.where((line == owner_x) & (lane == slot + 64), length_ref[item], tags)
-        return found + jnp.where(inside, 1, 0), tags
-
-    found, tags = lax.fori_loop(0, items, plan, (0, jnp.zeros((8, HEAD), jnp.int32)))
-    tail_copies = []
-    if tagging:
-        tags = tags.astype(jnp.float32)
-        for owner_x in range(sent_ref.shape[0]):
-            tagged[owner_x] = jnp.broadcast_to(tags[owner_x : owner_x + 1], (TAIL, HEAD)).astype(
-                jnp.bfloat16
-            )
-            tail_copies.append(
-                pltpu.make_async_copy(
-                    tagged.at[owner_x],
-                    sent_ref.at[owner_x, pl.ds((high - low) * rows, TAIL), pl.ds(0, HEAD)],
-                    tag_sem.at[owner_x],
-                )
-            )
-            tail_copies[-1].start()
-
-    def turn(step, carry):
-        for inner in range(TURN):
-            index = step * TURN + inner
-
-            @pl.when(index < found)
-            def _(index=index):
-                pltpu.make_async_copy(queries_ref.at[0], held.at[index], in_sems.at[index]).wait()
-
-        for inner in range(TURN):
-            index = step * TURN + inner
             for head in range(heads):
-                part = held[index, :, head * HEAD : (head + 1) * HEAD].astype(jnp.float32)
+                part = held[item, :, head * HEAD : (head + 1) * HEAD].astype(jnp.float32)
                 turned = part * tables[0] + pltpu.roll(part, HEAD // 2, 1) * tables[1]
-                staged[index, :, head * HEAD : (head + 1) * HEAD] = turned.astype(jnp.bfloat16)
-        for inner in range(TURN):
-            index = step * TURN + inner
-
-            @pl.when(index < found)
-            def _(index=index):
-                at = pl.ds(pl.multiple_of(to_slot_ref[index] * rows, rows), rows)
-                pltpu.make_async_copy(
-                    staged.at[index], sent_ref.at[to_x_ref[index], at], out_sems.at[index]
-                ).start()
-
-        return carry
-
-    lax.fori_loop(0, (found + TURN - 1) // TURN, turn, 0)
-
-    def leave(index, carry):
+                staged[item, :, head * HEAD : (head + 1) * HEAD] = turned.astype(jnp.bfloat16)
+        for item, shift, slot in routes:
+            for index, sent_ref in enumerate(sent_refs):
+                low, high = THERE[index // xs], THERE[index // xs + 1]
+
+                @pl.when((shift == index % xs) & (slot >= low) & (slot < high))
+                def _(item=item, slot=slot, low=low, sent_ref=sent_ref):
+                    at = pl.ds(pl.multiple_of((slot - low) * rows, rows), rows)
+                    pltpu.make_async_copy(
+                        staged.at[item], sent_ref.at[at], out_sems.at[item]
+                    ).start()
+
+        return tags
+
+    none = jnp.zeros((8, HEAD), jnp.int32)
+    tag_ref[...] = lax.fori_loop(0, items // TURN, turn, none)[:xs]
+    for item in range(items):
         pltpu.make_async_copy(
-            staged.at[index], sent_ref.at[0, pl.ds(0, rows)], out_sems.at[index]
+            staged.at[item], sent_refs[0].at[pl.ds(0, rows)], out_sems.at[item]
         ).wait()
-        return carry
-
-    lax.fori_loop(0, found, leave, 0)
-    for copy in tail_copies:
-        copy.wait()
-
-
-def attend_kernel(first_slot, sent_slot, tags_ref, sent_ref, after_ref, *refs):
+
+
+def attend_kernel(first_slot, skip, xs, x_ref, tags_ref, *refs):
+    sent_refs = refs[:xs]
     (
         *cache_refs, out_ref, held, staged, keys, values, even_scores, odd_scores,
         even_peak, odd_peak, at_ref, cache_ref, length_ref, in_sems, out_sems, cache_sems,
-    ) = refs
+    ) = refs[xs + 1 :]
     places = len(cache_refs) // 2
-    sources, slots = out_ref.shape[0], out_ref.shape[2]
+    my_x = x_ref[0]
+    sources, slots = out_ref.shape[1], out_ref.shape[2]
     rows, width = held.shape[1], held.shape[2]
     heads = width // HEAD
     parts = rows // 8
@@ -170,27 +140,26 @@
             )
             loads[-1].start()
 
-    def collect(index, found):
-        slot = index // sources
-        source = index - slot * sources
-        row = tags_ref[source, first_slot + slot]
-
-        @pl.when(row > 0)
-        def _():
-            pltpu.make_async_copy(
-                sent_ref.at[
-                    source, pl.ds(pl.multiple_of((slot + sent_slot) * rows, rows), rows)
-                ],
-                held.at[found],
-                in_sems.at[found],
-            ).start()
-            at_ref[found] = index
-            cache_ref[found] = slot // CAPC * CAPC + row - 1
-            length_ref[found] = tags_ref[source, 64 + first_slot + slot]
-
-        return found + jnp.where(row > 0, 1, 0)
-
-    found = lax.fori_loop(0, sources * slots, collect, 0)
+    def collect(slot, found):
+        for shift in range(xs):
+            source = lax.rem(my_x - shift + xs, xs)
+            row = tags_ref[source, first_slot + slot]
+
+            @pl.when(row > 0)
+            def _(shift=shift, source=source, row=row, found=found):
+                pltpu.make_async_copy(
+                    sent_refs[shift].at[pl.ds(pl.multiple_of((slot + skip) * rows, rows), rows)],
+                    held.at[found],
+                    in_sems.at[found],
+                ).start()
+                at_ref[found] = slot * sources + source
+                cache_ref[found] = slot // CAPC * CAPC + row - 1
+                length_ref[found] = tags_ref[source, 64 + first_slot + slot]
+
+            found = found + jnp.where(row > 0, 1, 0)
+        return found
+
+    found = lax.fori_loop(0, slots, collect, 0)
     for spare in range(2):
         cache_ref[found + spare] = 0
         length_ref[found + spare] = 0
@@ -198,7 +167,9 @@
         load.wait()
 
     def arrive(index, carry):
-        pltpu.make_async_copy(sent_ref.at[0, pl.ds(0, rows)], held.at[index], in_sems.at[index]).wait()
+        pltpu.make_async_copy(
+            sent_refs[0].at[pl.ds(0, rows)], held.at[index], in_sems.at[index]
+        ).wait()
         return carry
 
     lax.fori_loop(0, found, arrive, 0)
@@ -237,7 +208,7 @@
         at = at_ref[index]
         slot = at // sources
         pltpu.make_async_copy(
-            staged.at[index], out_ref.at[at - slot * sources, :, slot], out_sems.at[index]
+            staged.at[index], out_ref.at[:, at - slot * sources, slot], out_sems.at[index]
         ).start()
 
     score(0, even_scores, even_peak)
@@ -259,7 +230,7 @@
     lax.fori_loop(0, (found + 1) // 2, pair, 0)
 
     def leave(index, carry):
-        pltpu.make_async_copy(staged.at[index], out_ref.at[0, :, 0], out_sems.at[index]).wait()
+        pltpu.make_async_copy(staged.at[index], out_ref.at[:, 0, 0], out_sems.at[index]).wait()
         return carry
 
     lax.fori_loop(0, found, leave, 0)
@@ -270,7 +241,7 @@
     moved_refs = refs[:count]
     out_ref, held, slot_ref, prompt_ref, counts_ref, item_ref, in_sems, out_sems, sems = refs[-9:]
     items = held.shape[0]
-    columns, width = moved_refs[0].shape[1], moved_refs[0].shape[4]
+    columns, width = moved_refs[0].shape[0], moved_refs[0].shape[4]
     smalls = [
         pltpu.make_async_copy(slots_ref, slot_ref, sems.at[0]),
         pltpu.make_async_copy(prompts_ref, prompt_ref, sems.at[1]),
@@ -292,7 +263,7 @@
             def _(index=index, low=low):
                 for column in range(columns):
                     pltpu.make_async_copy(
-                        moved_refs[index].at[owner_x, column, slot - low],
+                        moved_refs[index].at[column, owner_x, slot - low],
                         held.at[found, :, pl.ds(column * width, width)],
                         in_sems.at[found],
                     ).start()
@@ -323,17 +294,21 @@
     return pl.BlockSpec(memory_space=pltpu.SMEM)
 
 
+def vmem():
+    return pl.BlockSpec(memory_space=pltpu.VMEM)
+
+
 def hbm():
     return pl.BlockSpec(memory_space=pltpu.HBM)
 
 
-def attend_call(tags, sent, used, first, count, ts=8, sent_slot=0, after=None):
-    xs, rows, width = sent.shape[0], 64, sent.shape[2]
+def attend_call(my_x, tags, sent, used, first, skip, count, rows, ts, after):
+    xs, width = len(sent), sent[0].shape[1]
     heads, prefix = width // HEAD, used[0][0].shape[1]
     return pl.pallas_call(
-        functools.partial(attend_kernel, first, sent_slot),
-        out_shape=jax.ShapeDtypeStruct((xs, ts, count, rows // ts, width), jnp.bfloat16),
-        in_specs=[smem(), hbm(), hbm()] + [hbm()] * (2 * len(used)),
+        functools.partial(attend_kernel, first, skip, xs),
+        out_shape=jax.ShapeDtypeStruct((ts, xs, count, rows // ts, width), jnp.bfloat16),
+        in_specs=[smem(), smem()] + [hbm()] * (xs + 1 + 2 * len(used)),
         out_specs=hbm(),
         scratch_shapes=[
             pltpu.VMEM((xs * count + 2, rows, width), jnp.bfloat16),
@@ -357,17 +332,14 @@
             bytes_accessed=4 * xs * count * rows * width,
             transcendentals=xs * count * rows * heads * prefix,
         ),
-    )(tags, sent, tags if after is None else after, *[c[0] for c in used], *[c[1] for c in used])
+    )(my_x, tags, *sent, after, *[c[0] for c in used], *[c[1] for c in used])
 
 
 def steps(queries, prefix_keys, prefix_values, slot_of_prompt, prompt_of, lengths):
     xs, zs, ts = lax.axis_size("x"), lax.axis_size("z"), lax.axis_size("t")
     items, rows, width = queries.shape
     prefix = prefix_keys.shape[1]
-    my_z = lax.axis_index("z").reshape(1)
-    slot_total = zs * CAPC
-    near_slots = NEAR * CAPC
-    far_slots = slot_total - near_slots
+    my_x, my_z = lax.axis_index("x").reshape(1), lax.axis_index("z").reshape(1)
 
     up = [(i, (i + 1) % zs) for i in range(zs)]
     down = [(i, (i - 1) % zs) for i in range(zs)]
@@ -381,59 +353,63 @@
         caches += [from_above[step], from_below[step]]
     caches.append(opposite)
 
-    tables = rotary_tables(prefix, rows)
-
-    def pack(low, high, tail):
-        return pl.pallas_call(
-            functools.partial(pack_kernel, low, high),
-            out_shape=jax.ShapeDtypeStruct(
-                (xs, (high - low) * rows + tail, width), jnp.bfloat16
-            ),
-            in_specs=[smem()] + [hbm()] * 5,
-            out_specs=hbm(),
-            scratch_shapes=[
-                pltpu.VMEM((items + TURN, rows, width), jnp.bfloat16),
-                pltpu.VMEM((items + TURN, rows, width), jnp.bfloat16),
-                pltpu.VMEM((2, rows, HEAD), jnp.float32),
-                pltpu.VMEM((xs, TAIL, HEAD), jnp.bfloat16),
-                pltpu.SMEM((xs * zs * CAPC,), jnp.int32),
-                pltpu.SMEM((items,), jnp.int32),
-                pltpu.SMEM((items,), jnp.int32),
-                pltpu.SMEM((xs * zs,), jnp.int32),
-                pltpu.SMEM((items,), jnp.int32),
-                pltpu.SMEM((items,), jnp.int32),
-                pltpu.SemaphoreType.DMA((items,)),
-                pltpu.SemaphoreType.DMA((items,)),
-                pltpu.SemaphoreType.DMA((4,)),
-                pltpu.SemaphoreType.DMA((xs,)),
-            ],
-            compiler_params=pltpu.CompilerParams(vmem_limit_bytes=VMEM),
-            cost_estimate=pl.CostEstimate(
-                flops=2 * 10**9, bytes_accessed=items * rows * width * 2, transcendentals=0
-            ),
-        )(my_z, slot_of_prompt, prompt_of, lengths, queries, tables)
-
-    near = pack(0, near_slots, TAIL)
-    far = pack(near_slots, slot_total, 0)
-    near = lax.all_to_all(near, "x", 0, 0, tiled=True)
-    far = lax.all_to_all(far, "x", 0, 0, tiled=True)
-    tags = near[:, near_slots * rows, :].astype(jnp.int32)[:, :HEAD]
-
-    def attend(sent, first, count, sent_slot, after):
+    *packed, tags = pl.pallas_call(
+        functools.partial(pack_kernel, xs),
+        out_shape=[
+            jax.ShapeDtypeStruct(((high - low) * rows, width), jnp.bfloat16)
+            for low, high in zip(THERE[:-1], THERE[1:])
+            for _ in range(xs)
+        ]
+        + [jax.ShapeDtypeStruct((xs, HEAD), jnp.int32)],
+        in_specs=[smem()] * 2 + [hbm()] * 5,
+        out_specs=[hbm()] * (xs * (len(THERE) - 1)) + [vmem()],
+        scratch_shapes=[
+            pltpu.VMEM((items, rows, width), jnp.bfloat16),
+            pltpu.VMEM((items, rows, width), jnp.bfloat16),
+            pltpu.VMEM((2, rows, HEAD), jnp.float32),
+            pltpu.SMEM((xs * zs * CAPC,), jnp.int32),
+            pltpu.SMEM((items,), jnp.int32),
+            pltpu.SMEM((items,), jnp.int32),
+            pltpu.SMEM((xs * zs,), jnp.int32),
+            pltpu.SemaphoreType.DMA((items,)),
+            pltpu.SemaphoreType.DMA((items,)),
+            pltpu.SemaphoreType.DMA((4,)),
+        ],
+        compiler_params=pltpu.CompilerParams(vmem_limit_bytes=VMEM),
+        cost_estimate=pl.CostEstimate(
+            flops=4 * 10**9, bytes_accessed=2 * items * rows * width * 2, transcendentals=0
+        ),
+    )(my_x, my_z, slot_of_prompt, prompt_of, lengths, queries, rotary_tables(prefix, rows))
+
+    def there(sent):
+        return [sent[0]] + [
+            lax.ppermute(sent[k], "x", [(i, (i + k) % xs) for i in range(xs)])
+            for k in range(1, xs)
+        ]
+
+    sent = []
+    for index in range(len(THERE) - 1):
+        sent.append(there(packed[index * xs : (index + 1) * xs]))
+    tags = lax.all_to_all(tags, "x", 0, 0, tiled=True)
+
+    def attend(first, count, after):
         used = caches[first // CAPC : (first + count) // CAPC]
-        return attend_call(tags, sent, used, first, count, ts, sent_slot, after)
+        part = sum(first >= low for low in THERE[1:])
+        return attend_call(
+            my_x, tags, sent[part], used, first, first - THERE[part], count, rows, ts, after
+        )
 
     def back(attended):
         shape = attended.shape
         moved = lax.all_to_all(
-            attended.reshape(xs * ts, *shape[2:]), ("x", "t"), 0, 0, tiled=True
+            attended.reshape(ts * xs, *shape[2:]), ("t", "x"), 0, 0, tiled=True
         )
         return moved.reshape(shape)
 
-    near = attend(near, 0, near_slots, 0, None)
-    far = attend(far, near_slots, far_slots, 0, near)
-    near = back(near)
-    far = back(far)
+    moved, after = [], tags
+    for low, high in zip(BOUNDS[:-1], BOUNDS[1:]):
+        after = attend(low, high - low, after)
+        moved.append(back(after))
 
     def join(bounds, moved, out):
         more = [] if out is None else [out]
@@ -459,8 +435,8 @@
             ),
         )(my_z, slot_of_prompt, prompt_of, *moved, *more)
 
-    out = join((0, near_slots), [near], None)
-    return join((near_slots, slot_total), [far], out)
+    out = join(BOUNDS[:-1], moved[:-1], None)
+    return join(BOUNDS[-2:], moved[-1:], out)
 
 
 def solution(mesh):

time: 204 us -> 225 us (1.10)
  blocking collectives: 0 us -> 36.3 us
  waiting for transfers between devices: 96.1 us -> 76.2 us
  starting transfers between devices: 57.9 us -> 62.5 us
    all_to_all x0 -> x2, blocking collectives: none -> 36.3 us  [the longest x1 28.6 us: back(): lax.all_to_all(attended.reshape(ts * xs, *shape[2:]), ('t', 'x'), 0, 0, t...]
    all_to_all x4 -> x2, waiting for transfers between devices: 47.4 us -> 20.9 us  [back(): lax.all_to_all(attended.reshape(ts * xs, *shape[2:]), ('t', 'x'), 0, 0, t...]
    ppermute x0 -> x6, waiting for transfers between devices: none -> 23.4 us  [there(): lax.ppermute(sent[k], 'x', [(i, (i + k) % xs) for i in range(xs)])]
    ppermute x6, waiting for transfers between devices: 23.4 us -> 8.92 us  [steps(): from_below.append(tuple((lax.ppermute(a, 'z', up) for a in from_below[-1])))]
    all_to_all x4 -> x2, starting transfers between devices: 30.1 us -> 15.9 us  [back(): lax.all_to_all(attended.reshape(ts * xs, *shape[2:]), ('t', 'x'), 0, 0, t...]
    ppermute x0 -> x6, starting transfers between devices: none -> 11.7 us  [there(): lax.ppermute(sent[k], 'x', [(i, (i + k) % xs) for i in range(xs)])]
    ppermute x6, starting transfers between devices: 0.61 us -> 4.5 us  [steps(): from_below.append(tuple((lax.ppermute(a, 'z', up) for a in from_below[-1])))]
    ppermute x6, waiting for transfers between devices: 14.1 us -> 11.6 us  [steps(): lax.ppermute(a, 'z', down)]
  transfers between devices with their start and end apart: 18 -> 22, of which waited for: 9 -> 10; matrix products, arithmetic and copies ran while one was open for 1% -> 0% of each run, Pallas kernels for 18% -> 12%
where the time goes in v2:
time: 225 us; the launch traced here: 223 us
  waiting for transfers between devices  76.2 us (34%)
  starting transfers between devices  62.5 us (28%)
  Pallas kernels  45.8 us (20%)
  blocking collectives  36.3 us (16%)
    pallas_call x3, Pallas kernels, attend_call(): pl.pallas_call(functools.partial(attend_kernel, first, skip, xs), out_sha...  31.3 us
    all_to_all x1, blocking collectives, back(): lax.all_to_all(attended.reshape(ts * xs, *shape[2:]), ('t', 'x'), 0, 0, t...  28.6 us
    ppermute x6, starting transfers between devices, steps(): lax.ppermute(a, 'z', down)  26.9 us
    ppermute x6, waiting for transfers between devices, there(): lax.ppermute(sent[k], 'x', [(i, (i + k) % xs) for i in range(xs)])  23.4 us
    all_to_all x2, waiting for transfers between devices, back(): lax.all_to_all(attended.reshape(ts * xs, *shape[2:]), ('t', 'x'), 0, 0, t...  20.9 us
    all_to_all x2, starting transfers between devices, back(): lax.all_to_all(attended.reshape(ts * xs, *shape[2:]), ('t', 'x'), 0, 0, t...  15.9 us
    ppermute x6, starting transfers between devices, there(): lax.ppermute(sent[k], 'x', [(i, (i + k) % xs) for i in range(xs)])  11.7 us
    ppermute x6, waiting for transfers between devices, steps(): lax.ppermute(a, 'z', down)  11.6 us
  transfers between devices with their start and end apart: 22, of which 10 were waited for; matrix products, arithmetic and copies ran while one was open for 0% of the time, Pallas kernels for 12%

profile of v2, /device:TPU:1, one launch (start us, length us, event | category | flops | bytes accessed | tf_op | source)
XLA Modules:
  0.0 222.7 jit_solution(11714410738287531055)
XLA Ops:
  0.0 5.9 %shard_map.73 = (bf16[384,640]{1,0:T(8,128)(2,1)}, bf16[384,640]{1,0:T(8,128)(2,1)}, bf16[384,640]{1,0:T(8,128)(2,1)}, bf16[384,640]{1,0:T(8,128)(2,1)}, bf16[64...) custom-call(s32[1]{0:T(128)} %bitcast.1.x_ref, ...), custom_call_target="tpu_custom_call" | custom-call | flops 4000000000 | bytes 5242880 | tf_op jit(solution)/shard_map/pallas_call | solution.py:356
  6.0 2.1 collective-permute-start.3
  8.1 2.5 %collective-permute-start.4 = (bf16[384,640]{1,0:T(8,128)(2,1)}, bf16[384,640]{1,0:T(8,128)(2,1)}, u32[]{:S(2)}, u32[]{:S(2)}) collective-permute-start(bf16[384,640]{1,0:T(8,128)(2,1)} %get-tuple-element.21), channel_id=1, source_target_pairs={{0,128},{64,192},{128,0},{192,64},{1,129},{65,193},{129,1},{193,65... | collective-permute-start | bytes 1474568 | tf_op jit(solution)/shard_map/ppermute | solution.py:386
  10.5 5.6 %collective-permute-start.6 = (bf16[2,1024,128]{2,1,0:T(8,128)(2,1)}, bf16[2,1024,128]{2,1,0:T(8,128)(2,1)}, u32[]{:S(2)}, u32[]{:S(2)}) collective-permute-start(bf16[2,1024,128]{2,1,0:T(8,128)(2,1)} %refs_5_.1), channel_id=1, source_target_pairs={{0,56},{8,0},{16,8},{24,16},{32,24},{40,32},{48,40},{56,48},{1,57}... | collective-permute-start | bytes 1572872 | tf_op jit(solution)/shard_map/ppermute | solution.py:349
  16.1 1.2 collective-permute-start.5
  17.3 0.0 collective-permute-start.7
  17.3 1.1 collective-permute-done.3.refs_1_
  18.4 1.9 collective-permute-start
  20.3 11.8 %collective-permute-done.4.refs_2_ = bf16[384,640]{1,0:T(8,128)(2,1)} collective-permute-done((bf16[384,640]{1,0:T(8,128)(2,1)}, bf16[384,640]{1,0:T(8,128)(2,1)}, u32[]{:S(2)}, u32[]{:S(2)}) %collective-permute-start.4) | collective-permute-done | bytes 491552 | tf_op jit(solution)/shard_map/ppermute | solution.py:386
  32.1 0.3 collective-permute-start.1
  32.4 0.0 collective-permute-done.5.refs_3_
  32.4 5.8 %collective-permute-start.8 = (bf16[2,1024,128]{2,1,0:T(8,128)(2,1)}, bf16[2,1024,128]{2,1,0:T(8,128)(2,1)}, u32[]{:S(2)}, u32[]{:S(2)}) collective-permute-start(bf16[2,1024,128]{2,1,0:T(8,128)(2,1)} %refs_8_.1), channel_id=1, source_target_pairs={{0,56},{8,0},{16,8},{24,16},{32,24},{40,32},{48,40},{56,48},{1,57}... | collective-permute-start | bytes 1572872 | tf_op jit(solution)/shard_map/ppermute | solution.py:349
  38.1 0.0 collective-permute-done.6.refs_6_
  38.2 0.0 collective-permute-start.9
  38.2 3.8 %collective-permute-start.2 = (bf16[640,640]{1,0:T(8,128)(2,1)}, bf16[640,640]{1,0:T(8,128)(2,1)}, u32[]{:S(2)}, u32[]{:S(2)}) collective-permute-start(bf16[640,640]{1,0:T(8,128)(2,1)} %get-tuple-element.18), channel_id=1, source_target_pairs={{0,192},{64,0},{128,64},{192,128},{1,193},{65,1},{129,65},{193,129... | collective-permute-start | bytes 2457608 | tf_op jit(solution)/shard_map/ppermute | solution.py:386
  42.0 4.8 %collective-permute-done.8.refs_9_ = bf16[2,1024,128]{2,1,0:T(8,128)(2,1)} collective-permute-done((bf16[2,1024,128]{2,1,0:T(8,128)(2,1)}, bf16[2,1024,128]{2,1,0:T(8,128)(2,1)}, u32[]{:S(2)}, u32[]{:S(2)}) %collective-permute-start.8) | collective-permute-done | bytes 524320 | tf_op jit(solution)/shard_map/ppermute | solution.py:349
  46.8 3.4 %collective-permute-start.10 = (bf16[2,1024,128]{2,1,0:T(8,128)(2,1)}, bf16[2,1024,128]{2,1,0:T(8,128)(2,1)}, u32[]{:S(2)}, u32[]{:S(2)}) collective-permute-start(bf16[2,1024,128]{2,1,0:T(8,128)(2,1)} %collective-permute-done.6.refs_6_), channel_id=1, source_target_pairs={{0,56},{8,0},{16,8},{24,16},{32,24},{40,32},{48,40},{56,48},{1,57}... | collective-permute-start | bytes 1572872 | tf_op jit(solution)/shard_map/ppermute | solution.py:349
  50.2 0.0 collective-permute-done.9.refs_10_
  50.2 0.0 collective-permute-start.11
  50.2 0.5 collective-permute-done.refs_1_
  50.7 6.4 %collective-permute-start.12 = (bf16[2,1024,128]{2,1,0:T(8,128)(2,1)}, bf16[2,1024,128]{2,1,0:T(8,128)(2,1)}, u32[]{:S(2)}, u32[]{:S(2)}) collective-permute-start(bf16[2,1024,128]{2,1,0:T(8,128)(2,1)} %collective-permute-done.8.refs_9_), channel_id=1, source_target_pairs={{0,56},{8,0},{16,8},{24,16},{32,24},{40,32},{48,40},{56,48},{1,57}... | collective-permute-start | bytes 1572872 | tf_op jit(solution)/shard_map/ppermute | solution.py:349
  57.2 10.0 %collective-permute-done.1.refs_2_ = bf16[640,640]{1,0:T(8,128)(2,1)} collective-permute-done((bf16[640,640]{1,0:T(8,128)(2,1)}, bf16[640,640]{1,0:T(8,128)(2,1)}, u32[]{:S(2)}, u32[]{:S(2)}) %collective-permute-start.1) | collective-permute-done | bytes 819232 | tf_op jit(solution)/shard_map/ppermute | solution.py:386
  67.2 1.6 collective-permute-start.13
  68.8 7.8 %all_to_all.26 = s32[4,1,128]{2,1,0:T(1,128)} all-to-all(s32[4,1,128]{2,1,0:T(1,128)} %bitcast.15), channel_id=1, replica_groups=mesh['x'=4,'z'=8,'t'=8] {'x'}, dimensions={0} | all-to-all | bytes 4096 | tf_op jit(solution)/shard_map/all_to_all | solution.py:393
  76.6 12.6 %shard_map.74.refs_4_ = bf16[8,4,6,8,640]{4,3,2,1,0:T(8,128)(2,1)} custom-call(s32[1]{0:T(128)} %bitcast.1.x_ref, s32[4,128]{1,0:T(4,128)} %bitcast.16, bf16[384,640]{1,0:T(8,128)(2,1)} %get-tuple-element.19.refs_0_, bf16[384,640]{1,0:T(8,128)(2,1)} %collective-permute-done.3.refs_1_, bf16[384,640]{1,0:T(8,128)(2,1)} %collective-permute-done.4.refs_2_, ...), custom_call_target="tpu_custom_call" | custom-call | flops 4026531840 | bytes 3932160 | tf_op jit(solution)/shard_map/pallas_call | solution.py:308
  89.2 0.0 collective-permute-done.11.refs_6_
  89.2 0.0 collective-permute-done.12.refs_7_
  89.2 8.5 %shard_map.75.refs_4_ = bf16[8,4,4,8,640]{4,3,2,1,0:T(8,128)(2,1)} custom-call(s32[1]{0:T(128)} %bitcast.1.x_ref, s32[4,128]{1,0:T(4,128)} %bitcast.18, bf16[640,640]{1,0:T(8,128)(2,1)} %get-tuple-element.15.refs_0_, bf16[640,640]{1,0:T(8,128)(2,1)} %collective-permute-done.refs_1_, bf16[640,640]{1,0:T(8,128)(2,1)} %collective-permute-done.1.refs_2_, ...), custom_call_target="tpu_custom_call" | custom-call | flops 2684354560 | bytes 2621440 | tf_op jit(solution)/shard_map/pallas_call | solution.py:308
  97.8 28.6 %all_to_all.27 = bf16[32,4,8,640]{3,2,1,0:T(8,128)(2,1)} all-to-all(bf16[32,4,8,640]{3,2,1,0:T(8,128)(2,1)} %bitcast.14), channel_id=1, replica_groups=mesh['x'=4,'z'=8,'t'=8] {'t','x'}, dimensions={0} | all-to-all | bytes 2621440 | tf_op jit(solution)/shard_map/all_to_all | solution.py:404
  126.3 4.6 %all-to-all-start.2 = ((bf16[32,6,8,640]{3,2,1,0:T(8,128)(2,1)}), bf16[32,6,8,640]{3,2,1,0:T(8,128)(2,1)}, u32[]{:S(2)}, u32[]{:S(2)}) async-start(bf16[32,6,8,640]{3,2,1,0:T(8,128)(2,1)} %bitcast.7), calls=%async_computation.2 | async-start | bytes 3932160 | tf_op jit(solution)/shard_map/all_to_all | solution.py:404
  130.9 2.9 %collective-permute-start.15 = (bf16[2,1024,128]{2,1,0:T(8,128)(2,1)}, bf16[2,1024,128]{2,1,0:T(8,128)(2,1)S(1)}, u32[]{:S(2)}, u32[]{:S(2)}) collective-permute-start(bf16[2,1024,128]{2,1,0:T(8,128)(2,1)} %collective-permute-done.11.refs_6_), channel_id=1, source_target_pairs={{0,8},{8,16},{16,24},{24,32},{32,40},{40,48},{48,56},{56,0},{1,9},... | collective-permute-start | bytes 1572872 | tf_op jit(solution)/shard_map/ppermute | solution.py:348
  133.8 2.4 %collective-permute-start.17 = (bf16[2,1024,128]{2,1,0:T(8,128)(2,1)}, bf16[2,1024,128]{2,1,0:T(8,128)(2,1)S(1)}, u32[]{:S(2)}, u32[]{:S(2)}) collective-permute-start(bf16[2,1024,128]{2,1,0:T(8,128)(2,1)} %collective-permute-done.12.refs_7_), channel_id=1, source_target_pairs={{0,56},{8,0},{16,8},{24,16},{32,24},{40,32},{48,40},{56,48},{1,57}... | collective-permute-start | bytes 1572872 | tf_op jit(solution)/shard_map/ppermute | solution.py:349
  136.2 3.3 %collective-permute-start.14 = (bf16[2,1024,128]{2,1,0:T(8,128)(2,1)}, bf16[2,1024,128]{2,1,0:T(8,128)(2,1)S(1)}, u32[]{:S(2)}, u32[]{:S(2)}) collective-permute-start(bf16[2,1024,128]{2,1,0:T(8,128)(2,1)} %collective-permute-done.10.refs_5_), channel_id=1, source_target_pairs={{0,56},{8,0},{16,8},{24,16},{32,24},{40,32},{48,40},{56,48},{1,57}... | collective-permute-start | bytes 1572872 | tf_op jit(solution)/shard_map/ppermute | solution.py:349
  139.5 8.7 %collective-permute-done.15.refs_6_ = bf16[2,1024,128]{2,1,0:T(8,128)(2,1)S(1)} collective-permute-done((bf16[2,1024,128]{2,1,0:T(8,128)(2,1)}, bf16[2,1024,128]{2,1,0:T(8,128)(2,1)S(1)}, u32[]{:S(2)}, u32[]{:S(2)}) %collective-permute-start.15) | collective-permute-done | bytes 524320 | tf_op jit(solution)/shard_map/ppermute | solution.py:348
  148.2 0.8 copy-done
  149.0 0.0 collective-permute-start.16
  149.0 0.0 collective-permute-done.17.refs_8_
  149.0 3.5 %collective-permute-start.19 = (bf16[2,1024,128]{2,1,0:T(8,128)(2,1)S(1)}, bf16[2,1024,128]{2,1,0:T(8,128)(2,1)}, u32[]{:S(2)}, u32[]{:S(2)}) collective-permute-start(bf16[2,1024,128]{2,1,0:T(8,128)(2,1)S(1)} %collective-permute-done.17.refs_8_), channel_id=1, source_target_pairs={{0,56},{8,0},{16,8},{24,16},{32,24},{40,32},{48,40},{56,48},{1,57}... | collective-permute-start | bytes 1572872 | tf_op jit(solution)/shard_map/ppermute | solution.py:350
  152.5 6.8 %collective-permute-done.14.refs_5_ = bf16[2,1024,128]{2,1,0:T(8,128)(2,1)S(1)} collective-permute-done((bf16[2,1024,128]{2,1,0:T(8,128)(2,1)}, bf16[2,1024,128]{2,1,0:T(8,128)(2,1)S(1)}, u32[]{:S(2)}, u32[]{:S(2)}) %collective-permute-start.14) | collective-permute-done | bytes 524320 | tf_op jit(solution)/shard_map/ppermute | solution.py:349
  159.3 0.2 collective-permute-done.18.refs_9_
  159.4 11.2 %collective-permute-done.16.refs_7_ = bf16[2,1024,128]{2,1,0:T(8,128)(2,1)S(1)} collective-permute-done((bf16[2,1024,128]{2,1,0:T(8,128)(2,1)S(1)}, bf16[2,1024,128]{2,1,0:T(8,128)(2,1)S(1)}, u32[]{:S(2)}, u32[]{:S(2)}) %collective-permute-start.16) | collective-permute-done | bytes 524320 | tf_op jit(solution)/shard_map/ppermute | solution.py:350
  170.7 0.8 copy-done.4
  171.5 0.0 collective-permute-done.19.refs_10_
  171.5 10.2 %shard_map.76 = bf16[8,4,6,8,640]{4,3,2,1,0:T(8,128)(2,1)} custom-call(s32[1]{0:T(128)} %bitcast.1.x_ref, s32[4,128]{1,0:T(4,128)} %bitcast.19, bf16[640,640]{1,0:T(8,128)(2,1)} %get-tuple-element.15.refs_0_, bf16[640,640]{1,0:T(8,128)(2,1)} %collective-permute-done.refs_1_, bf16[640,640]{1,0:T(8,128)(2,1)} %collective-permute-done.1.refs_2_, ...), custom_call_target="tpu_custom_call" | custom-call | flops 4026531840 | bytes 3932160 | tf_op jit(solution)/shard_map/pallas_call | solution.py:308
  181.7 11.3 %all-to-all-start.1 = ((bf16[32,6,8,640]{3,2,1,0:T(8,128)(2,1)}), bf16[32,6,8,640]{3,2,1,0:T(8,128)(2,1)}, u32[]{:S(2)}, u32[]{:S(2)}) async-start(bf16[32,6,8,640]{3,2,1,0:T(8,128)(2,1)} %bitcast.13), calls=%async_computation.1 | async-start | bytes 3932160 | tf_op jit(solution)/shard_map/all_to_all | solution.py:404
  193.1 4.6 %shard_map.77.refs_1_ = bf16[32,8,5120]{2,1,0:T(8,128)(2,1)} custom-call(s32[1]{0:T(128)} %bitcast.z_ref, s32[64]{0:T(128)} %slots_ref.5, s32[32]{0:T(128)} %prompts_ref.5, bf16[8,4,6,8,640]{4,3,2,1,0:T(8,128)(2,1)} %bitcast.8.refs_0_, bf16[8,4,4,8,640]{4,3,2,1,0:T(8,128)(2,1)} %bitcast.12), custom_call_target="tpu_custom_call" | custom-call | flops 1000000000 | bytes 2621440 | tf_op jit(solution)/shard_map/pallas_call | solution.py:416
  197.6 20.9 %all-to-all-done.1 = bf16[32,6,8,640]{3,2,1,0:T(8,128)(2,1)} async-done(((bf16[32,6,8,640]{3,2,1,0:T(8,128)(2,1)}), bf16[32,6,8,640]{3,2,1,0:T(8,128)(2,1)}, u32[]{:S(2)}, u32[]{:S(2)}) %all-to-all-start.1) | async-done | bytes 1966112 | tf_op jit(solution)/shard_map/all_to_all | solution.py:404
  218.5 3.9 %shard_map.78 = bf16[32,8,5120]{2,1,0:T(8,128)(2,1)} custom-call(s32[1]{0:T(128)} %bitcast.z_ref, s32[64]{0:T(128)} %slots_ref.5, s32[32]{0:T(128)} %prompts_ref.5, bf16[8,4,6,8,640]{4,3,2,1,0:T(8,128)(2,1)} %bitcast.6.refs_0_, bf16[32,8,5120]{2,1,0:T(8,128)(2,1)} %shard_map.77.refs_1_), custom_call_target="tpu_custom_call", output_to_operand_aliasing={{}: (4, {})} | custom-call | flops 1000000000 | bytes 2621440 | tf_op jit(solution)/shard_map/pallas_call | solution.py:416
  (14 shorter events, 0.0 us)
Async XLA Ops:
  6.0 12.5 %collective-permute-start.3 = (bf16[384,640]{1,0:T(8,128)(2,1)}, bf16[384,640]{1,0:T(8,128)(2,1)}, u32[]{:S(2)}, u32[]{:S(2)}) collective-permute-start(bf16[384,640]{1,0:T(8,128)(2,1)} %get-tuple-element.20), channel_id=1, source_target_pairs={{0,64},{64,128},{128,192},{192,0},{1,65},{65,129},{129,193},{193,1... | collective-permute-start | bytes 1474568 | tf_op jit(solution)/shard_map/ppermute | solution.py:386
  8.1 24.0 %collective-permute-start.4 = (bf16[384,640]{1,0:T(8,128)(2,1)}, bf16[384,640]{1,0:T(8,128)(2,1)}, u32[]{:S(2)}, u32[]{:S(2)}) collective-permute-start(bf16[384,640]{1,0:T(8,128)(2,1)} %get-tuple-element.21), channel_id=1, source_target_pairs={{0,128},{64,192},{128,0},{192,64},{1,129},{65,193},{129,1},{193,65... | collective-permute-start | bytes 1474568 | tf_op jit(solution)/shard_map/ppermute | solution.py:386
  10.5 27.6 %collective-permute-start.6 = (bf16[2,1024,128]{2,1,0:T(8,128)(2,1)}, bf16[2,1024,128]{2,1,0:T(8,128)(2,1)}, u32[]{:S(2)}, u32[]{:S(2)}) collective-permute-start(bf16[2,1024,128]{2,1,0:T(8,128)(2,1)} %refs_5_.1), channel_id=1, source_target_pairs={{0,56},{8,0},{16,8},{24,16},{32,24},{40,32},{48,40},{56,48},{1,57}... | collective-permute-start | bytes 1572872 | tf_op jit(solution)/shard_map/ppermute | solution.py:349
  16.1 16.3 %collective-permute-start.5 = (bf16[384,640]{1,0:T(8,128)(2,1)}, bf16[384,640]{1,0:T(8,128)(2,1)}, u32[]{:S(2)}, u32[]{:S(2)}) collective-permute-start(bf16[384,640]{1,0:T(8,128)(2,1)} %get-tuple-element.22), channel_id=1, source_target_pairs={{0,192},{64,0},{128,64},{192,128},{1,193},{65,1},{129,65},{193,129... | collective-permute-start | bytes 1474568 | tf_op jit(solution)/shard_map/ppermute | solution.py:386
  17.3 20.9 %collective-permute-start.7 = (bf16[2,1024,128]{2,1,0:T(8,128)(2,1)}, bf16[2,1024,128]{2,1,0:T(8,128)(2,1)}, u32[]{:S(2)}, u32[]{:S(2)}) collective-permute-start(bf16[2,1024,128]{2,1,0:T(8,128)(2,1)} %refs_5_.1), channel_id=1, source_target_pairs={{0,8},{8,16},{16,24},{24,32},{32,40},{40,48},{48,56},{56,0},{1,9},... | collective-permute-start | bytes 1572872 | tf_op jit(solution)/shard_map/ppermute | solution.py:348
  18.4 32.3 %collective-permute-start = (bf16[640,640]{1,0:T(8,128)(2,1)}, bf16[640,640]{1,0:T(8,128)(2,1)}, u32[]{:S(2)}, u32[]{:S(2)}) collective-permute-start(bf16[640,640]{1,0:T(8,128)(2,1)} %get-tuple-element.16), channel_id=1, source_target_pairs={{0,64},{64,128},{128,192},{192,0},{1,65},{65,129},{129,193},{193,1... | collective-permute-start | bytes 2457608 | tf_op jit(solution)/shard_map/ppermute | solution.py:386
  32.1 35.1 %collective-permute-start.1 = (bf16[640,640]{1,0:T(8,128)(2,1)}, bf16[640,640]{1,0:T(8,128)(2,1)}, u32[]{:S(2)}, u32[]{:S(2)}) collective-permute-start(bf16[640,640]{1,0:T(8,128)(2,1)} %get-tuple-element.17), channel_id=1, source_target_pairs={{0,128},{64,192},{128,0},{192,64},{1,129},{65,193},{129,1},{193,65... | collective-permute-start | bytes 2457608 | tf_op jit(solution)/shard_map/ppermute | solution.py:386
  32.4 14.5 %collective-permute-start.8 = (bf16[2,1024,128]{2,1,0:T(8,128)(2,1)}, bf16[2,1024,128]{2,1,0:T(8,128)(2,1)}, u32[]{:S(2)}, u32[]{:S(2)}) collective-permute-start(bf16[2,1024,128]{2,1,0:T(8,128)(2,1)} %refs_8_.1), channel_id=1, source_target_pairs={{0,56},{8,0},{16,8},{24,16},{32,24},{40,32},{48,40},{56,48},{1,57}... | collective-permute-start | bytes 1572872 | tf_op jit(solution)/shard_map/ppermute | solution.py:349
  38.2 12.1 %collective-permute-start.9 = (bf16[2,1024,128]{2,1,0:T(8,128)(2,1)}, bf16[2,1024,128]{2,1,0:T(8,128)(2,1)}, u32[]{:S(2)}, u32[]{:S(2)}) collective-permute-start(bf16[2,1024,128]{2,1,0:T(8,128)(2,1)} %refs_8_.1), channel_id=1, source_target_pairs={{0,8},{8,16},{16,24},{24,32},{32,40},{40,48},{48,56},{56,0},{1,9},... | collective-permute-start | bytes 1572872 | tf_op jit(solution)/shard_map/ppermute | solution.py:348
  38.2 51.0 %collective-permute-start.2 = (bf16[640,640]{1,0:T(8,128)(2,1)}, bf16[640,640]{1,0:T(8,128)(2,1)}, u32[]{:S(2)}, u32[]{:S(2)}) collective-permute-start(bf16[640,640]{1,0:T(8,128)(2,1)} %get-tuple-element.18), channel_id=1, source_target_pairs={{0,192},{64,0},{128,64},{192,128},{1,193},{65,1},{129,65},{193,129... | collective-permute-start | bytes 2457608 | tf_op jit(solution)/shard_map/ppermute | solution.py:386
  46.8 42.4 %collective-permute-start.10 = (bf16[2,1024,128]{2,1,0:T(8,128)(2,1)}, bf16[2,1024,128]{2,1,0:T(8,128)(2,1)}, u32[]{:S(2)}, u32[]{:S(2)}) collective-permute-start(bf16[2,1024,128]{2,1,0:T(8,128)(2,1)} %collective-permute-done.6.refs_6_), channel_id=1, source_target_pairs={{0,56},{8,0},{16,8},{24,16},{32,24},{40,32},{48,40},{56,48},{1,57}... | collective-permute-start | bytes 1572872 | tf_op jit(solution)/shard_map/ppermute | solution.py:349
  50.2 39.0 %collective-permute-start.11 = (bf16[2,1024,128]{2,1,0:T(8,128)(2,1)}, bf16[2,1024,128]{2,1,0:T(8,128)(2,1)}, u32[]{:S(2)}, u32[]{:S(2)}) collective-permute-start(bf16[2,1024,128]{2,1,0:T(8,128)(2,1)} %collective-permute-done.7.refs_7_), channel_id=1, source_target_pairs={{0,8},{8,16},{16,24},{24,32},{32,40},{40,48},{48,56},{56,0},{1,9},... | collective-permute-start | bytes 1572872 | tf_op jit(solution)/shard_map/ppermute | solution.py:348
  50.7 38.5 %collective-permute-start.12 = (bf16[2,1024,128]{2,1,0:T(8,128)(2,1)}, bf16[2,1024,128]{2,1,0:T(8,128)(2,1)}, u32[]{:S(2)}, u32[]{:S(2)}) collective-permute-start(bf16[2,1024,128]{2,1,0:T(8,128)(2,1)} %collective-permute-done.8.refs_9_), channel_id=1, source_target_pairs={{0,56},{8,0},{16,8},{24,16},{32,24},{40,32},{48,40},{56,48},{1,57}... | collective-permute-start | bytes 1572872 | tf_op jit(solution)/shard_map/ppermute | solution.py:349
  67.2 22.1 %collective-permute-start.13 = (bf16[2,1024,128]{2,1,0:T(8,128)(2,1)}, bf16[2,1024,128]{2,1,0:T(8,128)(2,1)}, u32[]{:S(2)}, u32[]{:S(2)}) collective-permute-start(bf16[2,1024,128]{2,1,0:T(8,128)(2,1)} %collective-permute-done.9.refs_10_), channel_id=1, source_target_pairs={{0,8},{8,16},{16,24},{24,32},{32,40},{40,48},{48,56},{56,0},{1,9},... | collective-permute-start | bytes 1572872 | tf_op jit(solution)/shard_map/ppermute | solution.py:348
  126.3 55.4 %all-to-all-start.2 = ((bf16[32,6,8,640]{3,2,1,0:T(8,128)(2,1)}), bf16[32,6,8,640]{3,2,1,0:T(8,128)(2,1)}, u32[]{:S(2)}, u32[]{:S(2)}) async-start(bf16[32,6,8,640]{3,2,1,0:T(8,128)(2,1)} %bitcast.7), calls=%async_computation.2 | async-start | bytes 3932160 | tf_op jit(solution)/shard_map/all_to_all | solution.py:404
  130.9 17.3 %collective-permute-start.15 = (bf16[2,1024,128]{2,1,0:T(8,128)(2,1)}, bf16[2,1024,128]{2,1,0:T(8,128)(2,1)S(1)}, u32[]{:S(2)}, u32[]{:S(2)}) collective-permute-start(bf16[2,1024,128]{2,1,0:T(8,128)(2,1)} %collective-permute-done.11.refs_6_), channel_id=1, source_target_pairs={{0,8},{8,16},{16,24},{24,32},{32,40},{40,48},{48,56},{56,0},{1,9},... | collective-permute-start | bytes 1572872 | tf_op jit(solution)/shard_map/ppermute | solution.py:348
  133.8 15.2 %collective-permute-start.17 = (bf16[2,1024,128]{2,1,0:T(8,128)(2,1)}, bf16[2,1024,128]{2,1,0:T(8,128)(2,1)S(1)}, u32[]{:S(2)}, u32[]{:S(2)}) collective-permute-start(bf16[2,1024,128]{2,1,0:T(8,128)(2,1)} %collective-permute-done.12.refs_7_), channel_id=1, source_target_pairs={{0,56},{8,0},{16,8},{24,16},{32,24},{40,32},{48,40},{56,48},{1,57}... | collective-permute-start | bytes 1572872 | tf_op jit(solution)/shard_map/ppermute | solution.py:349
  136.2 23.1 %collective-permute-start.14 = (bf16[2,1024,128]{2,1,0:T(8,128)(2,1)}, bf16[2,1024,128]{2,1,0:T(8,128)(2,1)S(1)}, u32[]{:S(2)}, u32[]{:S(2)}) collective-permute-start(bf16[2,1024,128]{2,1,0:T(8,128)(2,1)} %collective-permute-done.10.refs_5_), channel_id=1, source_target_pairs={{0,56},{8,0},{16,8},{24,16},{32,24},{40,32},{48,40},{56,48},{1,57}... | collective-permute-start | bytes 1572872 | tf_op jit(solution)/shard_map/ppermute | solution.py:349
  139.5 20.0 %collective-permute-start.18 = (bf16[2,1024,128]{2,1,0:T(8,128)(2,1)}, bf16[2,1024,128]{2,1,0:T(8,128)(2,1)S(1)}, u32[]{:S(2)}, u32[]{:S(2)}) collective-permute-start(bf16[2,1024,128]{2,1,0:T(8,128)(2,1)} %collective-permute-done.13.refs_8_), channel_id=1, source_target_pairs={{0,8},{8,16},{16,24},{24,32},{32,40},{40,48},{48,56},{56,0},{1,9},... | collective-permute-start | bytes 1572872 | tf_op jit(solution)/shard_map/ppermute | solution.py:348
  148.2 0.8 copy-start
  149.0 21.7 %collective-permute-start.16 = (bf16[2,1024,128]{2,1,0:T(8,128)(2,1)S(1)}, bf16[2,1024,128]{2,1,0:T(8,128)(2,1)S(1)}, u32[]{:S(2)}, u32[]{:S(2)}) collective-permute-start(bf16[2,1024,128]{2,1,0:T(8,128)(2,1)S(1)} %collective-permute-done.15.refs_6_), channel_id=1, source_target_pairs={{0,8},{8,16},{16,24},{24,32},{32,40},{40,48},{48,56},{56,0},{1,9},... | collective-permute-start | bytes 1572872 | tf_op jit(solution)/shard_map/ppermute | solution.py:350
  149.0 21.7 %copy-start.1 = (bf16[2,1024,128]{2,1,0:T(8,128)(2,1)}, bf16[2,1024,128]{2,1,0:T(8,128)(2,1)S(1)}, u32[]{:S(2)}) copy-start(bf16[2,1024,128]{2,1,0:T(8,128)(2,1)S(1)} %collective-permute-done.17.refs_8_) | copy-start | bytes 1572868
  149.0 22.5 %collective-permute-start.19 = (bf16[2,1024,128]{2,1,0:T(8,128)(2,1)S(1)}, bf16[2,1024,128]{2,1,0:T(8,128)(2,1)}, u32[]{:S(2)}, u32[]{:S(2)}) collective-permute-start(bf16[2,1024,128]{2,1,0:T(8,128)(2,1)S(1)} %collective-permute-done.17.refs_8_), channel_id=1, source_target_pairs={{0,56},{8,0},{16,8},{24,16},{32,24},{40,32},{48,40},{56,48},{1,57}... | collective-permute-start | bytes 1572872 | tf_op jit(solution)/shard_map/ppermute | solution.py:350
  159.3 11.4 %copy-start.2 = (bf16[2,1024,128]{2,1,0:T(8,128)(2,1)}, bf16[2,1024,128]{2,1,0:T(8,128)(2,1)S(1)}, u32[]{:S(2)}) copy-start(bf16[2,1024,128]{2,1,0:T(8,128)(2,1)S(1)} %collective-permute-done.14.refs_5_) | copy-start | bytes 1572868
  159.4 11.2 %copy-start.3 = (bf16[2,1024,128]{2,1,0:T(8,128)(2,1)}, bf16[2,1024,128]{2,1,0:T(8,128)(2,1)S(1)}, u32[]{:S(2)}) copy-start(bf16[2,1024,128]{2,1,0:T(8,128)(2,1)S(1)} %collective-permute-done.18.refs_9_) | copy-start | bytes 1572868
  170.7 0.8 copy-start.4
  181.7 36.8 %all-to-all-start.1 = ((bf16[32,6,8,640]{3,2,1,0:T(8,128)(2,1)}), bf16[32,6,8,640]{3,2,1,0:T(8,128)(2,1)}, u32[]{:S(2)}, u32[]{:S(2)}) async-start(bf16[32,6,8,640]{3,2,1,0:T(8,128)(2,1)} %bitcast.13), calls=%async_computation.1 | async-start | bytes 3932160 | tf_op jit(solution)/shard_map/all_to_all | solution.py:404
